TPU v7x, 256 devices: a whole 4x4x8 slice. The times are simulated.
256 devices in a mesh: gz: 128 (over x_lo, y, z, core), gy: 2 (over x_hi).
Axes of the slice: x: 4 (x_hi: 2, x_lo: 2; x = x_hi * 2 + x_lo), y: 4, z: 8, core: 2. Of those that a mesh axis runs over, the one named last changes fastest.
Arguments:
- fixed_image: float32 [1280, 80, 320], P('gz', 'gy'), may hold values from -6 to 6
- moving_image: float32 [1280, 80, 320], P('gz', 'gy'), may hold values from -6 to 6
- moving_grad: float32 [3, 1280, 80, 320], P(None, 'gz', 'gy'), may hold values from -6 to 6
Outputs:
- control_grad: float32 [256, 3, 16, 64], P('gz', None, 'gy')
All inputs are finite; a program needn't handle non-finite values.
Results may differ from a plain program's by a relative error of at most 0.00016.
Values sent between devices are 32-bit elements; how exact they have to be, the bound alone decides.
A program may use at most 64 MiB of HBM per device.

v0:
```python
import jax
import jax.numpy as jnp
from jax import lax
from jax.sharding import PartitionSpec as P

RADIUS = 4
SPACING = 5


EPS = 36.0
SIM_WEIGHT = 8.0


def passed_along(block, axis, distance):
    devices = range(lax.axis_size(axis))
    route = [(i - distance, i) for i in devices if i - distance in devices]
    return lax.ppermute(block, axis, route)


def in_blocks(shard, dim, count):
    shape = shard.shape
    blocks = shard.reshape(*shape[:dim], count, shape[dim] // count, *shape[dim + 1 :])
    return jnp.moveaxis(blocks, dim, 0)


def sum_at_owner(shard, axis, dim):
    count = lax.axis_size(axis)
    blocks = lax.all_to_all(in_blocks(shard, dim, count), axis, 0, 0, tiled=True)
    return jnp.sum(blocks, axis=0)


def padded(shard, sides, width):
    for axis, dim in sides:
        count, length = (lax.axis_size(axis), shard.shape[dim])
        up = [(i, (i + 1) % count) for i in range(count - 1)]
        down = [(j, i) for i, j in up]
        last = lax.slice_in_dim(shard, length - width, length, axis=dim)
        leading = lax.slice_in_dim(shard, 0, width, axis=dim)
        before = lax.ppermute(last, axis, up)
        after = lax.ppermute(leading, axis, down)
        shard = jnp.concatenate([before, shard, after], axis=dim)
    return shard


def spline_basis(voxels, points, anchor, first_point, columns):
    position = anchor + jnp.arange(voxels, dtype=jnp.int32)
    cell_index = position // SPACING
    fraction = (position - cell_index * SPACING).astype(jnp.float32) / SPACING
    remainder = 1.0 - fraction
    weights = [
        remainder**3 / 6.0,
        (3.0 * fraction**3 - 6.0 * fraction**2 + 4.0) / 6.0,
        (-3.0 * fraction**3 + 3.0 * fraction**2 + 3.0 * fraction + 1.0) / 6.0,
        fraction**3 / 6.0,
    ]
    targets = first_point + jnp.arange(columns, dtype=jnp.int32)
    matrix = jnp.zeros((voxels, columns), jnp.float32)
    for spline in range(4):
        clamped = jnp.clip(cell_index - 1 + spline, 0, points - 1)
        matrix = matrix + weights[spline][:, None] * (clamped[:, None] == targets[None, :]).astype(
            jnp.float32
        )
    return matrix


def box_along(values, dimension, length):
    running = lax.slice_in_dim(values, 0, length, axis=dimension)
    for offset in range(1, 2 * RADIUS + 1):
        running = running + lax.slice_in_dim(values, offset, offset + length, axis=dimension)
    return running


def box_three(values, plane_count, height):
    last_dim = values.ndim - 1
    widths = [(0, 0)] * last_dim + [(RADIUS, RADIUS)]
    summed = box_along(jnp.pad(values, widths), last_dim, values.shape[last_dim])
    summed = box_along(summed, last_dim - 1, height)
    return box_along(summed, last_dim - 2, plane_count)


def coefficient_fields(images):
    plane_count = images.shape[1] - 2 * RADIUS
    height = images.shape[2] - 2 * RADIUS
    fixed_part = images[0]
    moving_part = images[1]
    window_size = float((2 * RADIUS + 1) ** 3)
    sum_f = box_three(fixed_part, plane_count, height)
    sum_m = box_three(moving_part, plane_count, height)
    sum_ff = box_three(fixed_part * fixed_part, plane_count, height)
    sum_mm = box_three(moving_part * moving_part, plane_count, height)
    sum_fm = box_three(fixed_part * moving_part, plane_count, height)
    covariance = sum_fm - sum_f * sum_m / window_size
    variance_fixed = sum_ff - sum_f * sum_f / window_size + EPS
    variance_moving = sum_mm - sum_m * sum_m / window_size + EPS
    quotient = covariance / (variance_fixed * variance_moving)
    weight_cross = 2.0 * quotient
    weight_moving = -quotient * covariance / variance_moving
    return jnp.stack(
        [
            weight_cross,
            weight_cross * sum_f / window_size,
            weight_moving,
            weight_moving * sum_m / window_size,
        ]
    )


def from_neighbour(outgoing, offset):
    return passed_along(outgoing, "gz", offset)


def row_sum(partial_sums):
    return sum_at_owner(partial_sums, "gy", 2)


def combine_slabs(partial_sums, owned_points):
    result = partial_sums[1 : owned_points + 1]
    offsets = [-1, 1] + []
    for offset in offsets:
        if offset < 0:
            outgoing = partial_sums[0:1]
            target = owned_points - 1
        else:
            first_row = 1 + offset * owned_points
            last_row = min(owned_points + offset * owned_points, owned_points + 2)
            outgoing = partial_sums[first_row : last_row + 1]
            target = first_row - offset * owned_points - 1
        arrived = from_neighbour(outgoing, offset)
        result = result.at[target : target + arrived.shape[0]].add(arrived)
    return result


def local(fixed_image, moving_image, moving_grad):
    plane_count, height, widths = fixed_image.shape
    plane_base = lax.axis_index("gz") * plane_count
    row_base = lax.axis_index("gy") * height
    total_depth = plane_count * lax.axis_size("gz")
    total_height = height * lax.axis_size("gy")
    halo_depth = RADIUS
    stacked = jnp.stack([fixed_image, moving_image])
    images = padded(stacked, (("gz", 1), ("gy", 2)), halo_depth)
    coef_fields = coefficient_fields(images)
    coef_fields = padded(coef_fields, (("gz", 1), ("gy", 2)), RADIUS)
    boxed = box_three(coef_fields, plane_count, height)
    centre = images[:, halo_depth : halo_depth + plane_count, halo_depth : halo_depth + height]
    similarity_slope = -SIM_WEIGHT * (
        centre[0] * boxed[0] - boxed[1] + 2.0 * centre[1] * boxed[2] - 2.0 * boxed[3]
    )
    voxel_grad = similarity_slope[None] * moving_grad
    points_x = widths // SPACING
    basis_x = spline_basis(widths, points_x, 0, 0, points_x)
    along_x = jnp.dot(voxel_grad.reshape(-1, widths), basis_x, precision=lax.Precision.HIGHEST)
    along_x = along_x.reshape(3, plane_count, height, points_x)
    points_y = total_height // SPACING
    basis_y = spline_basis(height, points_y, row_base, 0, points_y)
    along_y = jnp.einsum("cdhx,hy->cdyx", along_x, basis_y, precision=lax.Precision.HIGHEST)
    owned_points = plane_count // SPACING
    basis_z = spline_basis(
        plane_count, total_depth // SPACING, plane_base, plane_base // SPACING - 1, owned_points + 3
    )
    partial_sums = jnp.einsum("cdyx,dq->qcyx", along_y, basis_z, precision=lax.Precision.HIGHEST)
    partial_sums = row_sum(partial_sums)
    result = combine_slabs(partial_sums, owned_points)
    return result


def solution(mesh):
    in_specs = (P("gz", "gy", None), P("gz", "gy", None), P(None, "gz", "gy", None))
    out_specs = P("gz", None, "gy", None)
    return jax.shard_map(local, mesh=mesh, in_specs=in_specs, out_specs=out_specs, check_vma=False)
```

profile of v0, /device:TPU:2, one launch (start us, length us, event | category | flops | bytes accessed | tf_op | source)
XLA Modules:
  0.0 161.0 jit_solution(17631009806443657430)
XLA Ops:
  1.5 1.9 %collective-permute-start = (f32[2,4,40,320]{3,2,1,0:T(8,128)S(1)}, f32[2,4,40,320]{3,2,1,0:T(8,128)S(1)}, u32[]{:S(2)}, u32[]{:S(2)}) collective-permute-start(f32[2,4,40,320]{3,2,1,0:T(8,128)S(1)} %get-tuple-element.56), channel_id=1, source_target_pairs={{0,2},{2,4},{4,6},{6,8},{8,10},{10,12},{12,14},{14,16},{16,18},{18... | collective-permute-start | bytes 1228808 | tf_op jit(solution)/shard_map/ppermute | solution.py:39
  3.4 9.6 %collective-permute-start.1 = (f32[2,4,40,320]{3,2,1,0:T(8,128)S(1)}, f32[2,4,40,320]{3,2,1,0:T(8,128)S(1)}, u32[]{:S(2)}, u32[]{:S(2)}) collective-permute-start(f32[2,4,40,320]{3,2,1,0:T(8,128)S(1)} %get-tuple-element.57), channel_id=1, source_target_pairs={{2,0},{4,2},{6,4},{8,6},{10,8},{12,10},{14,12},{16,14},{18,16},{20... | collective-permute-start | bytes 1228808 | tf_op jit(solution)/shard_map/ppermute | solution.py:40
  13.0 4.6 %collective-permute-done = f32[2,4,40,320]{3,2,1,0:T(8,128)S(1)} collective-permute-done((f32[2,4,40,320]{3,2,1,0:T(8,128)S(1)}, f32[2,4,40,320]{3,2,1,0:T(8,128)S(1)}, u32[]{:S(2)}, u32[]{:S(2)}) %collective-permute-start) | collective-permute-done | bytes 409632 | tf_op jit(solution)/shard_map/ppermute | solution.py:39
  19.5 4.3 %collective-permute-start.2 = (f32[2,18,4,320]{3,2,1,0:T(4,128)S(1)}, f32[2,18,4,320]{3,2,1,0:T(4,128)S(1)}, u32[]{:S(2)}, u32[]{:S(2)}) collective-permute-start(f32[2,18,4,320]{3,2,1,0:T(4,128)S(1)} %get-tuple-element.52), channel_id=1, source_target_pairs={{0,1},{2,3},{4,5},{6,7},{8,9},{10,11},{12,13},{14,15},{16,17},{18,... | collective-permute-start | bytes 552968 | tf_op jit(solution)/shard_map/ppermute | solution.py:39
  25.1 2.1 %collective-permute-done.2 = f32[2,18,4,320]{3,2,1,0:T(4,128)S(1)} collective-permute-done((f32[2,18,4,320]{3,2,1,0:T(4,128)S(1)}, f32[2,18,4,320]{3,2,1,0:T(4,128)S(1)}, u32[]{:S(2)}, u32[]{:S(2)}) %collective-permute-start.2) | collective-permute-done | bytes 184352 | tf_op jit(solution)/shard_map/ppermute | solution.py:39
  27.2 5.9 %collective-permute-done.3 = f32[2,18,4,320]{3,2,1,0:T(4,128)S(1)} collective-permute-done((f32[2,18,4,320]{3,2,1,0:T(4,128)S(1)}, f32[2,18,4,320]{3,2,1,0:T(4,128)S(1)}, u32[]{:S(2)}, u32[]{:S(2)}) %collective-permute-start.3) | collective-permute-done | bytes 184352 | tf_op jit(solution)/shard_map/ppermute | solution.py:40
  34.0 5.6 %slice_add_fusion.17 = (f32[18,48,320]{2,1,0:T(8,128)S(1)}, f32[18,48,320]{2,1,0:T(8,128)S(1)}) fusion(f32[18,48,320]{2,1,0:T(8,128)S(1)} %get-tuple-element.47, f32[18,48,320]{2,1,0:T(8,128)S(1)} %get-tuple-element.49), kind=kLoop, calls=%fused_computation.28 | loop fusion | flops 4423680 | bytes 4423680 | tf_op jit(solution)/shard_map/add | solution.py:69
  41.2 5.6 %slice_add_fusion.19 = (f32[18,48,320]{2,1,0:T(8,128)S(1)}, f32[18,48,320]{2,1,0:T(8,128)S(1)}) fusion(f32[18,48,320]{2,1,0:T(8,128)S(1)} %get-tuple-element.45, f32[18,48,320]{2,1,0:T(8,128)S(1)} %get-tuple-element.46), kind=kLoop, calls=%fused_computation.40 | loop fusion | flops 4423680 | bytes 4423680 | tf_op jit(solution)/shard_map/add | solution.py:69
  48.4 2.8 %slice_add_fusion.21 = f32[18,48,320]{2,1,0:T(8,128)S(1)} fusion(f32[18,48,320]{2,1,0:T(8,128)S(1)} %get-tuple-element.48), kind=kLoop, calls=%fused_computation.52 | loop fusion | flops 2211840 | bytes 2211840 | tf_op jit(solution)/shard_map/add | solution.py:69
  52.0 2.6 %multiply_bitcast_fusion.2 = (f32[1,10,40,320]{3,2,1,0:T(8,128)S(1)}, f32[10,40,320]{2,1,0:T(8,128)S(1)}, f32[10,40,320]{2,1,0:T(8,128)S(1)}, f32[10,40,320]{2,1...) fusion(f32[18,40,320]{2,1,0:T(8,128)S(1)} %slice_add_fusion.30, ...), kind=kLoop, calls=%fused_computation.164 | loop fusion | flops 6912000 | bytes 26112000 | tf_op jit(solution)/shard_map/stack | solution.py:98
  56.4 1.9 %collective-permute-start.4 = (f32[4,4,40,320]{3,2,1,0:T(8,128)}, f32[4,4,40,320]{3,2,1,0:T(8,128)}, u32[]{:S(2)}, u32[]{:S(2)}) collective-permute-start(f32[4,4,40,320]{3,2,1,0:T(8,128)} %get-tuple-element.50), channel_id=1, source_target_pairs={{0,2},{2,4},{4,6},{6,8},{8,10},{10,12},{12,14},{14,16},{16,18},{18... | collective-permute-start | bytes 2457608 | tf_op jit(solution)/shard_map/ppermute | solution.py:39
  58.3 7.9 %collective-permute-start.5 = (f32[4,4,40,320]{3,2,1,0:T(8,128)}, f32[4,4,40,320]{3,2,1,0:T(8,128)}, u32[]{:S(2)}, u32[]{:S(2)}) collective-permute-start(f32[4,4,40,320]{3,2,1,0:T(8,128)} %get-tuple-element.51), channel_id=1, source_target_pairs={{2,0},{4,2},{6,4},{8,6},{10,8},{12,10},{14,12},{16,14},{18,16},{20... | collective-permute-start | bytes 2457608 | tf_op jit(solution)/shard_map/ppermute | solution.py:40
  66.4 9.9 %collective-permute-done.4 = f32[4,4,40,320]{3,2,1,0:T(8,128)} collective-permute-done((f32[4,4,40,320]{3,2,1,0:T(8,128)}, f32[4,4,40,320]{3,2,1,0:T(8,128)}, u32[]{:S(2)}, u32[]{:S(2)}) %collective-permute-start.4) | collective-permute-done | bytes 819232 | tf_op jit(solution)/shard_map/ppermute | solution.py:39
  76.3 1.8 %collective-permute-done.5 = f32[4,4,40,320]{3,2,1,0:T(8,128)} collective-permute-done((f32[4,4,40,320]{3,2,1,0:T(8,128)}, f32[4,4,40,320]{3,2,1,0:T(8,128)}, u32[]{:S(2)}, u32[]{:S(2)}) %collective-permute-start.5) | collective-permute-done | bytes 819232 | tf_op jit(solution)/shard_map/ppermute | solution.py:40
  82.4 4.4 %collective-permute-done.6 = f32[4,18,4,320]{3,2,1,0:T(4,128)S(1)} collective-permute-done((f32[4,18,4,320]{3,2,1,0:T(4,128)S(1)}, f32[4,18,4,320]{3,2,1,0:T(4,128)S(1)}, u32[]{:S(2)}, u32[]{:S(2)}) %collective-permute-start.6) | collective-permute-done | bytes 368672 | tf_op jit(solution)/shard_map/ppermute | solution.py:39
  86.8 5.9 %collective-permute-done.7 = f32[4,18,4,320]{3,2,1,0:T(4,128)S(1)} collective-permute-done((f32[4,18,4,320]{3,2,1,0:T(4,128)S(1)}, f32[4,18,4,320]{3,2,1,0:T(4,128)S(1)}, u32[]{:S(2)}, u32[]{:S(2)}) %collective-permute-start.7) | collective-permute-done | bytes 368672 | tf_op jit(solution)/shard_map/ppermute | solution.py:40
  92.7 5.8 %pad_maximum_fusion = f32[4,18,48,320]{3,2,1,0:T(8,128)} fusion(f32[4,18,4,320]{3,2,1,0:T(4,128)S(1)} %collective-permute-done.7, f32[4,4,40,320]{3,2,1,0:T(8,128)} %collective-permute-done.5, f32[1,10,40,320]{3,2,1,0:T(8,128)S(1)} %get-tuple-element.55, f32[1,10,40,320]{3,2,1,0:T(8,128)S(1)} %get-tuple-element.54, f32[1,10,40,320]{3,2,1,0:T(8,128)S(1)} %copy-done.3, ...), kind=kLoop, calls=%fused_computation | loop fusion | flops 7741440 | bytes 8847360 | tf_op jit(solution)/shard_map/concatenate | solution.py:41
  98.6 22.2 %slice_add_fusion = f32[4,18,48,320]{3,2,1,0:T(8,128)S(1)} fusion(f32[4,18,48,320]{3,2,1,0:T(8,128)} %pad_maximum_fusion), kind=kLoop, calls=%fused_computation.1 | loop fusion | flops 8847360 | bytes 8847360 | tf_op jit(solution)/shard_map/add | solution.py:69
  120.7 4.6 %slice_add_fusion.1 = f32[4,18,40,320]{3,2,1,0:T(8,128)} fusion(f32[4,18,48,320]{3,2,1,0:T(8,128)S(1)} %slice_add_fusion), kind=kLoop, calls=%fused_computation.7 | loop fusion | flops 7372800 | bytes 36864000 | tf_op jit(solution)/shard_map/add | solution.py:69
  125.3 9.6 %slice_add_fusion.9 = f32[4,10,40,320]{3,2,1,0:T(8,128)S(1)} fusion(f32[4,18,40,320]{3,2,1,0:T(8,128)} %slice_add_fusion.1), kind=kLoop, calls=%fused_computation.16 | loop fusion | flops 4096000 | bytes 20480000 | tf_op jit(solution)/shard_map/add | solution.py:69
  136.4 2.0 %fusion.2 = f32[3,10,40,64]{3,2,1,0:T(8,128)S(1)} fusion(f32[3,10,40,320]{3,2,1,0:T(8,128)S(1)} %copy-done.4, f32[10,40,320]{2,1,0:T(8,128)S(1)} %fusion.17, f32[320]{0:T(512)S(1)} %get-tuple-element.70, s32[320]{0:T(512)S(1)} %get-tuple-element.71, f32[320]{0:T(512)S(1)} %get-tuple-element.68, s32[320]{0:T(512)S(1)} %get-tuple-element.72, ...), kind=kOutput, calls=%fused_computation.24 | convolution fusion | flops 295521280 | bytes 2365440 | tf_op jit(solution)/shard_map/dot_general | solution.py:152
  139.5 8.0 %all_to_all.5 = f32[2,1,7680]{2,1,0:T(1,128)S(1)} all-to-all(f32[2,1,7680]{2,1,0:T(1,128)S(1)} %reshape.268), channel_id=1, replica_groups=mesh['gz'=128,'gy'=2] {'gy'}, dimensions={0} | all-to-all | bytes 122880 | tf_op jit(solution)/shard_map/all_to_all | solution.py:28
  149.0 1.9 %collective-permute-start.9 = (f32[2,3,8,64]{3,0,2,1:T(2,128)S(1)}, f32[2,3,8,64]{3,0,2,1:T(2,128)S(1)}, u32[]{:S(2)}, u32[]{:S(2)}) collective-permute-start(f32[2,3,8,64]{3,0,2,1:T(2,128)S(1)} %copy.15), channel_id=1, source_target_pairs={{0,2},{2,4},{4,6},{6,8},{8,10},{10,12},{12,14},{14,16},{16,18},{18... | collective-permute-start | bytes 36872 | tf_op jit(solution)/shard_map/ppermute | solution.py:17
  151.0 7.9 %collective-permute-start.8 = (f32[1,3,8,64]{3,0,2,1:T(1,128)S(1)}, f32[1,3,8,64]{3,0,2,1:T(1,128)S(1)}, u32[]{:S(2)}, u32[]{:S(2)}) collective-permute-start(f32[1,3,8,64]{3,0,2,1:T(1,128)S(1)} %bitcast.82), channel_id=1, source_target_pairs={{2,0},{4,2},{6,4},{8,6},{10,8},{12,10},{14,12},{16,14},{18,16},{20... | collective-permute-start | bytes 18440 | tf_op jit(solution)/shard_map/ppermute | solution.py:17
  (59 shorter events, 21.8 us)
Async XLA Ops:
  0.0 19.4 %copy-start.1 = (f32[10,40,320]{2,1,0:T(8,128)S(1)}, f32[10,40,320]{2,1,0:T(8,128)}, u32[]{:S(2)}) copy-start(f32[10,40,320]{2,1,0:T(8,128)} %param.9) | copy-start | bytes 1536004
  0.0 19.4 %copy-start = (f32[10,40,320]{2,1,0:T(8,128)S(1)}, f32[10,40,320]{2,1,0:T(8,128)}, u32[]{:S(2)}) copy-start(f32[10,40,320]{2,1,0:T(8,128)} %param.10) | copy-start | bytes 1536004
  1.5 16.1 %collective-permute-start = (f32[2,4,40,320]{3,2,1,0:T(8,128)S(1)}, f32[2,4,40,320]{3,2,1,0:T(8,128)S(1)}, u32[]{:S(2)}, u32[]{:S(2)}) collective-permute-start(f32[2,4,40,320]{3,2,1,0:T(8,128)S(1)} %get-tuple-element.56), channel_id=1, source_target_pairs={{0,2},{2,4},{4,6},{6,8},{8,10},{10,12},{12,14},{14,16},{16,18},{18... | collective-permute-start | bytes 1228808 | tf_op jit(solution)/shard_map/ppermute | solution.py:39
  3.4 16.0 %collective-permute-start.1 = (f32[2,4,40,320]{3,2,1,0:T(8,128)S(1)}, f32[2,4,40,320]{3,2,1,0:T(8,128)S(1)}, u32[]{:S(2)}, u32[]{:S(2)}) collective-permute-start(f32[2,4,40,320]{3,2,1,0:T(8,128)S(1)} %get-tuple-element.57), channel_id=1, source_target_pairs={{2,0},{4,2},{6,4},{8,6},{10,8},{12,10},{14,12},{16,14},{18,16},{20... | collective-permute-start | bytes 1228808 | tf_op jit(solution)/shard_map/ppermute | solution.py:40
  19.5 7.8 %collective-permute-start.2 = (f32[2,18,4,320]{3,2,1,0:T(4,128)S(1)}, f32[2,18,4,320]{3,2,1,0:T(4,128)S(1)}, u32[]{:S(2)}, u32[]{:S(2)}) collective-permute-start(f32[2,18,4,320]{3,2,1,0:T(4,128)S(1)} %get-tuple-element.52), channel_id=1, source_target_pairs={{0,1},{2,3},{4,5},{6,7},{8,9},{10,11},{12,13},{14,15},{16,17},{18,... | collective-permute-start | bytes 552968 | tf_op jit(solution)/shard_map/ppermute | solution.py:39
  23.8 9.3 %collective-permute-start.3 = (f32[2,18,4,320]{3,2,1,0:T(4,128)S(1)}, f32[2,18,4,320]{3,2,1,0:T(4,128)S(1)}, u32[]{:S(2)}, u32[]{:S(2)}) collective-permute-start(f32[2,18,4,320]{3,2,1,0:T(4,128)S(1)} %get-tuple-element.53), channel_id=1, source_target_pairs={{1,0},{3,2},{5,4},{7,6},{9,8},{11,10},{13,12},{15,14},{17,16},{19,... | collective-permute-start | bytes 552968 | tf_op jit(solution)/shard_map/ppermute | solution.py:40
  54.9 1.5 copy-start.2
  56.4 19.9 %collective-permute-start.4 = (f32[4,4,40,320]{3,2,1,0:T(8,128)}, f32[4,4,40,320]{3,2,1,0:T(8,128)}, u32[]{:S(2)}, u32[]{:S(2)}) collective-permute-start(f32[4,4,40,320]{3,2,1,0:T(8,128)} %get-tuple-element.50), channel_id=1, source_target_pairs={{0,2},{2,4},{4,6},{6,8},{8,10},{10,12},{12,14},{14,16},{16,18},{18... | collective-permute-start | bytes 2457608 | tf_op jit(solution)/shard_map/ppermute | solution.py:39
  58.3 19.8 %collective-permute-start.5 = (f32[4,4,40,320]{3,2,1,0:T(8,128)}, f32[4,4,40,320]{3,2,1,0:T(8,128)}, u32[]{:S(2)}, u32[]{:S(2)}) collective-permute-start(f32[4,4,40,320]{3,2,1,0:T(8,128)} %get-tuple-element.51), channel_id=1, source_target_pairs={{2,0},{4,2},{6,4},{8,6},{10,8},{12,10},{14,12},{16,14},{18,16},{20... | collective-permute-start | bytes 2457608 | tf_op jit(solution)/shard_map/ppermute | solution.py:40
  66.4 26.4 %copy-start.3 = (f32[1,10,40,320]{3,2,1,0:T(8,128)S(1)}, f32[1,10,40,320]{3,2,1,0:T(8,128)}, u32[]{:S(2)}) copy-start(f32[1,10,40,320]{3,2,1,0:T(8,128)} %copy-done.2) | copy-start | bytes 1536004
  79.5 7.3 %collective-permute-start.6 = (f32[4,18,4,320]{3,2,1,0:T(4,128)S(1)}, f32[4,18,4,320]{3,2,1,0:T(4,128)S(1)}, u32[]{:S(2)}, u32[]{:S(2)}) collective-permute-start(f32[4,18,4,320]{3,2,1,0:T(4,128)S(1)} %get-tuple-element.43), channel_id=1, source_target_pairs={{0,1},{2,3},{4,5},{6,7},{8,9},{10,11},{12,13},{14,15},{16,17},{18,... | collective-permute-start | bytes 1105928 | tf_op jit(solution)/shard_map/ppermute | solution.py:39
  81.0 11.7 %collective-permute-start.7 = (f32[4,18,4,320]{3,2,1,0:T(4,128)S(1)}, f32[4,18,4,320]{3,2,1,0:T(4,128)S(1)}, u32[]{:S(2)}, u32[]{:S(2)}) collective-permute-start(f32[4,18,4,320]{3,2,1,0:T(4,128)S(1)} %get-tuple-element.44), channel_id=1, source_target_pairs={{1,0},{3,2},{5,4},{7,6},{9,8},{11,10},{13,12},{15,14},{17,16},{19,... | collective-permute-start | bytes 1105928 | tf_op jit(solution)/shard_map/ppermute | solution.py:40
  134.9 1.5 copy-start.4
  149.0 11.3 %collective-permute-start.9 = (f32[2,3,8,64]{3,0,2,1:T(2,128)S(1)}, f32[2,3,8,64]{3,0,2,1:T(2,128)S(1)}, u32[]{:S(2)}, u32[]{:S(2)}) collective-permute-start(f32[2,3,8,64]{3,0,2,1:T(2,128)S(1)} %copy.15), channel_id=1, source_target_pairs={{0,2},{2,4},{4,6},{6,8},{8,10},{10,12},{12,14},{14,16},{16,18},{18... | collective-permute-start | bytes 36872 | tf_op jit(solution)/shard_map/ppermute | solution.py:17
  151.0 9.3 %collective-permute-start.8 = (f32[1,3,8,64]{3,0,2,1:T(1,128)S(1)}, f32[1,3,8,64]{3,0,2,1:T(1,128)S(1)}, u32[]{:S(2)}, u32[]{:S(2)}) collective-permute-start(f32[1,3,8,64]{3,0,2,1:T(1,128)S(1)} %bitcast.82), channel_id=1, source_target_pairs={{2,0},{4,2},{6,4},{8,6},{10,8},{12,10},{14,12},{16,14},{18,16},{20... | collective-permute-start | bytes 18440 | tf_op jit(solution)/shard_map/ppermute | solution.py:17
where the time goes:
time: 161 us
  other arithmetic  69.5 us (43%)
  starting transfers between devices  39.5 us (25%)
  waiting for transfers between devices  37.7 us (23%)
  blocking collectives  7.98 us (5%)
  local copies, waits for them, and re-layouts  2.98 us (2%)
  matrix products  2.94 us (2%)
    add x11, other arithmetic, box_along(): running + lax.slice_in_dim(values, offset, offset + length, axis=dimension)  54.3 us
    ppermute x4, waiting for transfers between devices, padded(): before = lax.ppermute(last, axis, up)  21 us
    ppermute x4, starting transfers between devices, padded(): after = lax.ppermute(leading, axis, down)  20.1 us
    ppermute x4, waiting for transfers between devices, padded(): after = lax.ppermute(leading, axis, down)  15.3 us
    ppermute x2, starting transfers between devices, passed_along(): return lax.ppermute(block, axis, route)  9.78 us
    ppermute x4, starting transfers between devices, padded(): before = lax.ppermute(last, axis, up)  9.64 us
    all_to_all x1, blocking collectives, sum_at_owner(): lax.all_to_all(in_blocks(shard, dim, count), axis, 0, 0, tiled=True)  7.98 us
    concatenate x2, other arithmetic, padded(): shard = jnp.concatenate([before, shard, after], axis=dim)  6.15 us
  transfers between devices with their start and end apart: 10, of which 9 were waited for; matrix products, arithmetic and copies ran while one was open for 0% of the time, Pallas kernels for 0%

commit v1 on v0

v1 whole, which is shorter than its diff:
```python
import functools

import jax
import jax.numpy as jnp
import numpy as np
from jax import lax
from jax.experimental import pallas as pl
from jax.experimental.pallas import tpu as pltpu
from jax.sharding import PartitionSpec as P

RADIUS = 4
SPACING = 5
EPS = 36.0
SIM_WEIGHT = 8.0
WINDOW = float((2 * RADIUS + 1) ** 3)
MESH = pl.DeviceIdType.MESH

PLANES = 10
ROWS = 40
NX = 320
POINTS = 64
HALO = 2 * RADIUS
RAW_PLANES = PLANES + 2 * HALO
RAW_ROWS = ROWS + 2 * HALO
COEF_PLANES = PLANES + 2 * RADIUS
COEF_ROWS = ROWS + 2 * RADIUS
PAIRS = (0, 8, 2, 6, 4)


def spline_weights(step):
    u = step / SPACING
    return (
        (1.0 - u) ** 3 / 6.0,
        (3.0 * u**3 - 6.0 * u**2 + 4.0) / 6.0,
        (-3.0 * u**3 + 3.0 * u**2 + 3.0 * u + 1.0) / 6.0,
        u**3 / 6.0,
    )


def basis_along_x():
    matrix = np.zeros((384, 128), np.float64)
    for x in range(NX):
        for k, weight in enumerate(spline_weights(x % SPACING)):
            point = min(max(x // SPACING - 1 + k, 0), POINTS - 1)
            matrix[x, point] += weight
    matrix = matrix.astype(np.float32)
    high = matrix.astype(jnp.bfloat16)
    low = (matrix - high.astype(np.float32)).astype(jnp.bfloat16)
    return high, low


def suffix_sums(values):
    sums = [values[-1]]
    for value in reversed(values[:-1]):
        sums.append(sums[-1] + value)
    return sums[::-1]


def prefix_sums(values):
    sums = [values[0]]
    for value in values[1:]:
        sums.append(sums[-1] + value)
    return sums


def windows_of_nine(values):
    count = len(values) - 8
    if count > 9:
        before = suffix_sums(values[:9])
        after = prefix_sums(values[9:])
        return [before[0]] + [before[i] + after[i - 1] for i in range(1, 9)] + [after[8]]
    common = values[count - 1]
    for value in values[count:9]:
        common = common + value
    before = suffix_sums(values[: count - 1])
    after = prefix_sums(values[9:])
    out = []
    for i in range(count):
        total = common
        if i < count - 1:
            total = total + before[i]
        if i > 0:
            total = total + after[i - 1]
        out.append(total)
    return out


def box_along_x(tiles, lane):
    def shifted(parts, amount):
        turned = [pltpu.roll(part, amount % 128, 1) for part in parts]
        if amount > 0:
            return [jnp.where(lane < amount, turned[i - 1], turned[i]) for i in range(3)]
        return [jnp.where(lane >= 128 + amount, turned[(i + 1) % 3], turned[i]) for i in range(3)]

    three = [a + b + c for a, b, c in zip(tiles, shifted(tiles, 1), shifted(tiles, -1))]
    return [a + b + c for a, b, c in zip(three, shifted(three, 3), shifted(three, -3))]


def kernel(
    depth, f_hbm, m_hbm, g_hbm, bh_hbm, bl_hbm, out_ref,
    raw, f_tail, m_tail, grad, g_tail, bh, bl, own_sum, halo_sum, zsum, coef, zcoef, weighted, wide,
    sums, from_next, from_prev, from_side, from_next_side, from_prev_side,
    local_sem, y_send, y_recv, z_send, z_recv, s_send, s_recv, e_send, e_recv,
):
    gz = lax.axis_index("gz")
    gy = lax.axis_index("gy")
    other = 1 - gy
    is_first = gz == 0
    is_last = gz == depth - 1
    before = (jnp.maximum(gz - 1, 0), gy)
    after = (jnp.minimum(gz + 1, depth - 1), gy)
    before_side = (jnp.maximum(gz - 1, 0), other)
    after_side = (jnp.minimum(gz + 1, depth - 1), other)
    side = (gz, other)

    local = []

    def bring(src, dst):
        copy = pltpu.make_async_copy(src, dst, local_sem.at[len(local)])
        copy.start()
        local.append(copy)

    own = pl.ds(HALO, PLANES)
    rows_own = pl.ds(HALO, ROWS)
    bring(f_hbm.at[:, :, pl.ds(256, 64)], f_tail)
    bring(m_hbm.at[:, :, pl.ds(256, 64)], m_tail)
    for t in range(2):
        bring(f_hbm.at[:, :, pl.ds(128 * t, 128)], raw.at[t, own, rows_own, :])
        bring(m_hbm.at[:, :, pl.ds(128 * t, 128)], raw.at[2 + t, own, rows_own, :])
    for t in range(2):
        bring(g_hbm.at[:, :, :, pl.ds(128 * t, 128)], grad.at[t])
    bring(g_hbm.at[:, :, :, pl.ds(256, 64)], g_tail)
    bring(bh_hbm, bh)
    bring(bl_hbm, bl)

    barrier = pltpu.get_barrier_semaphore()
    pl.semaphore_signal(barrier, inc=1, device_id=side, device_id_type=MESH)

    @pl.when(jnp.logical_not(is_first))
    def _():
        pl.semaphore_signal(barrier, inc=1, device_id=before, device_id_type=MESH)
        pl.semaphore_signal(barrier, inc=1, device_id=before_side, device_id_type=MESH)

    @pl.when(jnp.logical_not(is_last))
    def _():
        pl.semaphore_signal(barrier, inc=1, device_id=after, device_id_type=MESH)
        pl.semaphore_signal(barrier, inc=1, device_id=after_side, device_id_type=MESH)

    lane = lax.broadcasted_iota(jnp.int32, (8, 128), 1)
    row = lax.broadcasted_iota(jnp.int32, (8, 128), 0)
    zero = jnp.zeros((8, 128), jnp.float32)
    low_half = lane < 64

    zero_row = pl.multiple_of(48 * gy, 8)
    strip_row = pl.multiple_of(48 - 48 * gy, 8)
    zsum[:, pl.ds(zero_row, 8), :] = jnp.zeros((26, 8, 128), jnp.float32)
    halo_sum[...] = jnp.zeros_like(halo_sum)

    local[0].wait()
    local[1].wait()
    for z in range(PLANES):
        raw[4, HALO + z, HALO : HALO + ROWS, :] = jnp.concatenate([f_tail[z], m_tail[z]], axis=-1)
    for copy in local[2:6]:
        copy.wait()

    @pl.when(is_first | is_last)
    def _():
        pl.semaphore_wait(barrier, 3)

    @pl.when(jnp.logical_not(is_first | is_last))
    def _():
        pl.semaphore_wait(barrier, 5)

    src_row = pl.multiple_of(40 - 32 * gy, 8)
    y_copies = []
    for i, first in enumerate(PAIRS):
        copy = pltpu.make_async_remote_copy(
            src_ref=raw.at[:, pl.ds(HALO + first, 2), pl.ds(src_row, 8), :],
            dst_ref=raw.at[:, pl.ds(HALO + first, 2), pl.ds(zero_row, 8), :],
            send_sem=y_send.at[i], recv_sem=y_recv.at[i], device_id=side, device_id_type=MESH,
        )
        copy.start()
        y_copies.append(copy)

    def to_after(k, rows, send, recv):
        return pltpu.make_async_remote_copy(
            src_ref=raw.at[:, pl.ds(16 - 2 * k, 2), rows, :],
            dst_ref=raw.at[:, pl.ds(6 - 2 * k, 2), rows, :],
            send_sem=send.at[0, k], recv_sem=recv.at[0, k], device_id=after, device_id_type=MESH,
        )

    def to_before(k, rows, send, recv):
        return pltpu.make_async_remote_copy(
            src_ref=raw.at[:, pl.ds(8 + 2 * k, 2), rows, :],
            dst_ref=raw.at[:, pl.ds(18 + 2 * k, 2), rows, :],
            send_sem=send.at[1, k], recv_sem=recv.at[1, k], device_id=before, device_id_type=MESH,
        )

    strip = pl.ds(strip_row, 8)

    def start_planes(k, rows, send, recv):
        @pl.when(jnp.logical_not(is_last))
        def _():
            to_after(k, rows, send, recv).start()

        @pl.when(jnp.logical_not(is_first))
        def _():
            to_before(k, rows, send, recv).start()

    def wait_planes(k, rows, send, recv):
        @pl.when(jnp.logical_not(is_first))
        def _():
            to_after(k, rows, send, recv).wait_recv()

        @pl.when(jnp.logical_not(is_last))
        def _():
            to_before(k, rows, send, recv).wait_recv()

    def wait_sent(k, rows, send, recv):
        @pl.when(jnp.logical_not(is_last))
        def _():
            to_after(k, rows, send, recv).wait_send()

        @pl.when(jnp.logical_not(is_first))
        def _():
            to_before(k, rows, send, recv).wait_send()

    for k in range(3):
        start_planes(k, rows_own, z_send, z_recv)

    @pl.when(is_first)
    def _():
        raw[:, 0:HALO, :, :] = jnp.zeros((5, HALO, RAW_ROWS, 128), jnp.float32)

    @pl.when(is_last)
    def _():
        raw[:, HALO + PLANES : RAW_PLANES, :, :] = jnp.zeros((5, HALO, RAW_ROWS, 128), jnp.float32)

    def fields_of(plane, rows):
        out = []
        for t in range(2):
            f = raw[t, plane, rows, :]
            m = raw[2 + t, plane, rows, :]
            out += [f, m, f * f, m * m, f * m]
        p = raw[4, plane, rows, :]
        return out + [p, p * p, p * pltpu.roll(p, 64, 1)]

    def own_windows(rows):
        columns = [fields_of(HALO + z, rows) for z in range(PLANES)]
        for col in range(13):
            values = [columns[z][col] for z in range(PLANES)]
            for p, total in enumerate(prefix_sums(values[:9])):
                own_sum[col, p, rows, :] = total
            for p, total in enumerate(suffix_sums(values[1:])):
                own_sum[col, 9 + p, rows, :] = total

    @pl.loop(0, 5)
    def _(i):
        own_windows(pl.ds(pl.multiple_of(8 + 8 * i, 8), 8))

    y_copies[0].wait_recv()
    y_copies[1].wait_recv()
    start_planes(0, strip, s_send, s_recv)
    start_planes(3, rows_own, z_send, z_recv)
    y_copies[2].wait_recv()
    y_copies[3].wait_recv()
    start_planes(1, strip, s_send, s_recv)
    y_copies[4].wait_recv()
    start_planes(2, strip, s_send, s_recv)
    start_planes(3, strip, s_send, s_recv)
    own_windows(strip)

    row_valid = []
    for j in range(6):
        position = 6 * row + j + 40 * gy - 4
        row_valid.append(jnp.where((position >= 0) & (position < 80), 1.0, 0.0))

    groups = [pl.ds(8 + 8 * i, 8) for i in range(5)] + [strip]

    def coefficients(planes, halo):
        for s in range(2):
            for rows in groups:
                if halo is None:
                    for col in range(13):
                        zsum[13 * s + col, rows, :] = own_sum[col, planes[s], rows, :]
                else:
                    fields = fields_of(halo[s], rows)
                    for col in range(13):
                        total = halo_sum[s, col, rows, :] + fields[col]
                        halo_sum[s, col, rows, :] = total
                        zsum[13 * s + col, rows, :] = total + own_sum[col, planes[s], rows, :]
        for s in range(2):
            position = gz * PLANES + planes[s] - RADIUS
            inside = jnp.where((position >= 0) & (position < depth * PLANES), 1.0, 0.0)
            summed = []
            for col in range(13):
                summed.append(windows_of_nine([zsum[13 * s + col, pl.ds(m, 8, stride=6), :] for m in range(14)]))
            for j in range(6):
                v = [summed[col][j] for col in range(13)]
                tail, square = pltpu.roll(v[10], 64, 1), pltpu.roll(v[11], 64, 1)
                last = [jnp.where(low_half, a, 0.0) for a in (v[10], tail, v[11], square, v[12])]
                boxed = [box_along_x([v[i], v[5 + i], last[i]], lane) for i in range(5)]
                valid = row_valid[j] * inside
                for t in range(3):
                    sf, sm, sff, smm, sfm = [boxed[i][t] for i in range(5)]
                    mf = sf * (1.0 / WINDOW)
                    mm = sm * (1.0 / WINDOW)
                    a = (sfm - mf * sm) * (valid if t < 2 else jnp.where(low_half, valid, 0.0))
                    p = sff - mf * sf + EPS
                    q = smm - mm * sm + EPS
                    r = 1.0 / (p * q)
                    cross = a * r
                    moving = -cross * a * (r * p)
                    where = pl.ds(j, 8, stride=6)
                    coef[t, planes[s], where, :] = cross
                    coef[3 + t, planes[s], where, :] = moving
                    coef[6 + t, planes[s], where, :] = cross * mf + moving * mm

    coefficients((8, 9), None)

    @pl.loop(0, 4)
    def _(k):
        wait_planes(k, rows_own, z_send, z_recv)
        wait_planes(k, strip, s_send, s_recv)

        @pl.loop(0, 2)
        def _(half):
            step = 2 * k + half
            coefficients((7 - step, 10 + step), (7 - step, 18 + step))

    for copy in local[6:]:
        copy.wait()
    grad[2] = jnp.concatenate([g_tail[...], jnp.zeros_like(g_tail)], axis=-1)

    @pl.loop(0, 9)
    def _(col):
        for g in range(6):
            rows = pl.ds(8 * g, 8)
            for z, total in enumerate(windows_of_nine([coef[col, p, rows, :] for p in range(COEF_PLANES)])):
                zcoef[col, z, rows, :] = total

    def slope_plane(z):
        summed = []
        for col in range(9):
            summed.append(windows_of_nine([zcoef[col, z, pl.ds(m, 8, stride=5), :] for m in range(13)]))
        for j in range(5):
            boxed = [box_along_x([summed[3 * i + t][j] for t in range(3)], lane) for i in range(3)]
            centre = pl.ds(HALO + j, 8, stride=5)
            tail = raw[4, HALO + z, centre, :]
            f = [raw[0, HALO + z, centre, :], raw[1, HALO + z, centre, :], tail]
            m = [raw[2, HALO + z, centre, :], raw[3, HALO + z, centre, :], pltpu.roll(tail, 64, 1)]
            for t in range(3):
                slope = f[t] * boxed[0][t] + m[t] * boxed[1][t] - boxed[2][t]
                for c in range(3):
                    weighted[c, t, j, z] = slope * grad[t, c, z, pl.ds(j, 8, stride=5), :]

    @pl.loop(0, 5)
    def _(z):
        slope_plane(z)
        slope_plane(z + 5)

    wy = [spline_weights(j) for j in range(SPACING)]
    wz = [[-2.0 * SIM_WEIGHT * w for w in ws] for ws in wy]
    for t in range(3):
        @pl.loop(0, 3)
        def _(c):
            slots = []
            for j in range(SPACING):
                v = [weighted[c, t, j, z] for z in range(PLANES)]
                part = []
                for i in range(2):
                    for k in range(4):
                        total = wz[0][k] * v[5 * i]
                        for step in range(1, SPACING):
                            if wz[step][k] != 0.0:
                                total = total + wz[step][k] * v[5 * i + step]
                        part.append(total)
                slots.append([part[0], part[1] + part[4], part[2] + part[5], part[3] + part[6], part[7]])
            for m in range(5):
                y = []
                for k in range(4):
                    total = wy[0][k] * slots[0][m]
                    for j in range(1, SPACING):
                        total = total + wy[j][k] * slots[j][m]
                    y.append(total)
                r0, r2, r3 = pltpu.roll(y[0], 7, 0), pltpu.roll(y[2], 1, 0), pltpu.roll(y[3], 2, 0)
                inner = (
                    jnp.where(row == 7, 0.0, r0) + y[1] + jnp.where(row == 0, 0.0, r2) + jnp.where(row < 2, 0.0, r3)
                )
                to_low = jnp.where(row == 7, r0, 0.0)
                to_high = jnp.where(row == 0, r2, 0.0) + jnp.where(row < 2, r3, 0.0)
                clip_low = jnp.where(row == 0, y[0], 0.0)
                clip_high = jnp.where(row == 7, y[2] + y[3] + pltpu.roll(y[3], 1, 0), 0.0)
                is_low = gy == 0
                base = pl.multiple_of(48 * m + 8 * c, 8)
                lanes = pl.ds(128 * t, 128)
                wide[pl.ds(base, 8), lanes] = inner + jnp.where(is_low, clip_low, clip_high)
                wide[pl.ds(pl.multiple_of(base + 24, 8), 8), lanes] = jnp.where(is_low, to_high, to_low)

    left = wide[...]
    high = left.astype(jnp.bfloat16)
    low = (left - high.astype(jnp.float32)).astype(jnp.bfloat16)

    def dot(a, b):
        return jnp.dot(a, b, preferred_element_type=jnp.float32)

    total = dot(high, bh[...]) + (dot(low, bh[...]) + dot(high, bl[...]))
    sums[...] = total.reshape(5, 2, 3, 8, 128)

    copies = [
        (0, sums.at[0, 0], from_next, before, 0),
        (0, sums.at[0, 1], from_next_side, before_side, 1),
        (1, sums.at[pl.ds(3, 2), 0], from_prev, after, 2),
        (1, sums.at[pl.ds(3, 2), 1], from_prev_side, after_side, 3),
    ]
    rdmas = [
        (
            direction,
            pltpu.make_async_remote_copy(
                src_ref=src, dst_ref=dst, send_sem=e_send.at[i], recv_sem=e_recv.at[i],
                device_id=target, device_id_type=MESH,
            ),
        )
        for direction, src, dst, target, i in copies
    ]
    side_copy = pltpu.make_async_remote_copy(
        src_ref=sums.at[pl.ds(1, 2), 1], dst_ref=from_side, send_sem=e_send.at[4], recv_sem=e_recv.at[4],
        device_id=side, device_id_type=MESH,
    )

    @pl.when(jnp.logical_not(is_first))
    def _():
        for direction, copy in rdmas:
            if direction == 0:
                copy.start()

    @pl.when(jnp.logical_not(is_last))
    def _():
        for direction, copy in rdmas:
            if direction == 1:
                copy.start()

    low_clip = jnp.where(is_first, 1.0, 0.0)
    high_clip = jnp.where(is_last, 1.0, 0.0)
    sums[1] = sums[1] + low_clip * sums[0]
    sums[2] = sums[2] + high_clip * (sums[3] + sums[4])
    side_copy.start()

    @pl.when(is_last)
    def _():
        from_next[...] = jnp.zeros_like(from_next)
        from_next_side[...] = jnp.zeros_like(from_next_side)

    @pl.when(is_first)
    def _():
        from_prev[...] = jnp.zeros_like(from_prev)
        from_prev_side[...] = jnp.zeros_like(from_prev_side)

    @pl.when(jnp.logical_not(is_last))
    def _():
        for direction, copy in rdmas:
            if direction == 0:
                copy.wait_recv()

    @pl.when(jnp.logical_not(is_first))
    def _():
        for direction, copy in rdmas:
            if direction == 1:
                copy.wait_recv()

    side_copy.wait_recv()
    first = sums[1, 0] + from_side[0] + from_prev[0] + from_prev_side[0]
    second = sums[2, 0] + from_side[1] + from_prev[1] + from_prev_side[1] + from_next[...] + from_next_side[...]
    out_ref[0] = first[:, :, :POINTS]
    out_ref[1] = second[:, :, :POINTS]

    for copy in y_copies:
        copy.wait_send()
    for k in range(4):
        wait_sent(k, rows_own, z_send, z_recv)
        wait_sent(k, strip, s_send, s_recv)
    side_copy.wait_send()

    @pl.when(jnp.logical_not(is_first))
    def _():
        for direction, copy in rdmas:
            if direction == 0:
                copy.wait_send()

    @pl.when(jnp.logical_not(is_last))
    def _():
        for direction, copy in rdmas:
            if direction == 1:
                copy.wait_send()


def local_gradient(depth, fixed_image, moving_image, moving_grad):
    high, low = basis_along_x()
    f32 = jnp.float32
    anywhere = pl.BlockSpec(memory_space=pl.ANY)
    dma = pltpu.SemaphoreType.DMA
    return pl.pallas_call(
        functools.partial(kernel, depth),
        out_shape=jax.ShapeDtypeStruct((2, 3, 8, POINTS), f32),
        in_specs=[anywhere] * 5,
        out_specs=pl.BlockSpec(memory_space=pltpu.VMEM),
        scratch_shapes=[
            pltpu.VMEM((5, RAW_PLANES, RAW_ROWS, 128), f32),
            pltpu.VMEM((PLANES, ROWS, 64), f32),
            pltpu.VMEM((PLANES, ROWS, 64), f32),
            pltpu.VMEM((3, 3, PLANES, ROWS, 128), f32),
            pltpu.VMEM((3, PLANES, ROWS, 64), f32),
            pltpu.VMEM((384, 128), jnp.bfloat16),
            pltpu.VMEM((384, 128), jnp.bfloat16),
            pltpu.VMEM((13, COEF_PLANES, RAW_ROWS, 128), f32),
            pltpu.VMEM((2, 13, RAW_ROWS, 128), f32),
            pltpu.VMEM((26, RAW_ROWS, 128), f32),
            pltpu.VMEM((9, COEF_PLANES, COEF_ROWS, 128), f32),
            pltpu.VMEM((9, PLANES, COEF_ROWS, 128), f32),
            pltpu.VMEM((3, 3, 5, PLANES, 8, 128), f32),
            pltpu.VMEM((240, 384), f32),
            pltpu.VMEM((5, 2, 3, 8, 128), f32),
            pltpu.VMEM((3, 8, 128), f32),
            pltpu.VMEM((2, 3, 8, 128), f32),
            pltpu.VMEM((2, 3, 8, 128), f32),
            pltpu.VMEM((3, 8, 128), f32),
            pltpu.VMEM((2, 3, 8, 128), f32),
            dma((11,)),
            dma((5,)),
            dma((5,)),
            dma((2, 4)),
            dma((2, 4)),
            dma((2, 4)),
            dma((2, 4)),
            dma((5,)),
            dma((5,)),
        ],
        compiler_params=pltpu.CompilerParams(collective_id=0, has_side_effects=True, vmem_limit_bytes=60 * 1024 * 1024),
    )(fixed_image, moving_image, moving_grad, high, low)


def solution(mesh):
    in_specs = (P("gz", "gy", None), P("gz", "gy", None), P(None, "gz", "gy", None))
    out_specs = P("gz", None, "gy", None)
    body = functools.partial(local_gradient, mesh.shape["gz"])
    return jax.shard_map(body, mesh=mesh, in_specs=in_specs, out_specs=out_specs, check_vma=False)
```

time: 161 us -> 74.9 us (0.47)
  the two profiles are of different devices: /device:TPU:2 before, /device:TPU:24 now
where the time goes in v1:
time: 74.9 us; the launch traced here: 74.8 us
  Pallas kernels  73.4 us (98%)
  local copies, waits for them, and re-layouts  1.35 us (2%)
    pallas_call x1, Pallas kernels, local_gradient(): pl.pallas_call(functools.partial(kernel, depth), out_shape=jax.ShapeDtype...  73.4 us

profile of v1, /device:TPU:24, one launch (start us, length us, event | category | flops | bytes accessed | tf_op | source)
XLA Modules:
  0.0 74.8 jit_solution(2967254830670590488)
XLA Ops:
  0.0 73.4 %shard_map.55 = f32[2,3,8,64]{3,2,1,0:T(8,128)} custom-call(f32[10,40,320]{2,1,0:T(8,128)} %f_hbm.1, f32[10,40,320]{2,1,0:T(8,128)} %m_hbm.1, f32[3,10,40,320]{3,2,1,0:T(8,128)} %g_hbm.1, bf16[384,128]{1,0:T(8,128)(2,1)} %constant.4.clone.bh_hbm, bf16[384,128]{1,0:T(8,128)(2,1)} %constant.5.clone.bl_hbm), custom_call_target="tpu_custom_call" | custom-call | tf_op jit(solution)/shard_map/pallas_call | solution.py:502
  73.4 1.3 %copy.7 = f32[2,3,8,64]{3,2,1,0:T(8,128)} copy(f32[2,3,8,64]{3,2,1,0:T(8,128)} %shard_map.55) | data formatting | bytes 24576

commit v2 on v1

--- a/solution.py
+++ b/solution.py
@@ -85,20 +85,20 @@
     return out
 
 
-def box_along_x(tiles, lane):
-    def shifted(parts, amount):
-        turned = [pltpu.roll(part, amount % 128, 1) for part in parts]
-        if amount > 0:
-            return [jnp.where(lane < amount, turned[i - 1], turned[i]) for i in range(3)]
-        return [jnp.where(lane >= 128 + amount, turned[(i + 1) % 3], turned[i]) for i in range(3)]
-
-    three = [a + b + c for a, b, c in zip(tiles, shifted(tiles, 1), shifted(tiles, -1))]
-    return [a + b + c for a, b, c in zip(three, shifted(three, 3), shifted(three, -3))]
+def three_along_x(tiles, reach, lane):
+    right = [pltpu.roll(tile, reach, 1) for tile in tiles]
+    left = [pltpu.roll(tile, 128 - reach, 1) for tile in tiles]
+    out = []
+    for i in range(3):
+        before = jnp.where(lane < reach, right[i - 1], right[i])
+        after = jnp.where(lane >= 128 - reach, left[(i + 1) % 3], left[i])
+        out.append(tiles[i] + before + after)
+    return out
 
 
 def kernel(
     depth, f_hbm, m_hbm, g_hbm, bh_hbm, bl_hbm, out_ref,
-    raw, f_tail, m_tail, grad, g_tail, bh, bl, own_sum, halo_sum, zsum, coef, zcoef, weighted, wide,
+    raw, f_tail, m_tail, grad, g_tail, bh, bl, own_sum, halo_sum, zsum, stage_y, stage_x, coef, zcoef, weighted, wide,
     sums, from_next, from_prev, from_side, from_next_side, from_prev_side,
     local_sem, y_send, y_recv, z_send, z_recv, s_send, s_recv, e_send, e_recv,
 ):
@@ -290,16 +290,27 @@
                         halo_sum[s, col, rows, :] = total
                         zsum[13 * s + col, rows, :] = total + own_sum[col, planes[s], rows, :]
         for s in range(2):
+            for col in range(13):
+                total = windows_of_nine([zsum[13 * s + col, pl.ds(m, 8, stride=6), :] for m in range(14)])
+                for j in range(6):
+                    if col < 10:
+                        stage_y[s, j, 3 * (col % 5) + col // 5] = total[j]
+                    elif col == 12:
+                        stage_y[s, j, 14] = jnp.where(low_half, total[j], 0.0)
+                    else:
+                        stage_y[s, j, 6 * (col - 10) + 2] = jnp.where(low_half, total[j], 0.0)
+                        stage_y[s, j, 6 * (col - 10) + 5] = jnp.where(low_half, pltpu.roll(total[j], 64, 1), 0.0)
+        for s in range(2):
+            for j in range(6):
+                for i in range(5):
+                    three = three_along_x([stage_y[s, j, 3 * i + t] for t in range(3)], 1, lane)
+                    for t in range(3):
+                        stage_x[s, j, 3 * i + t] = three[t]
+        for s in range(2):
             position = gz * PLANES + planes[s] - RADIUS
             inside = jnp.where((position >= 0) & (position < depth * PLANES), 1.0, 0.0)
-            summed = []
-            for col in range(13):
-                summed.append(windows_of_nine([zsum[13 * s + col, pl.ds(m, 8, stride=6), :] for m in range(14)]))
             for j in range(6):
-                v = [summed[col][j] for col in range(13)]
-                tail, square = pltpu.roll(v[10], 64, 1), pltpu.roll(v[11], 64, 1)
-                last = [jnp.where(low_half, a, 0.0) for a in (v[10], tail, v[11], square, v[12])]
-                boxed = [box_along_x([v[i], v[5 + i], last[i]], lane) for i in range(5)]
+                boxed = [three_along_x([stage_x[s, j, 3 * i + t] for t in range(3)], 3, lane) for i in range(5)]
                 valid = row_valid[j] * inside
                 for t in range(3):
                     sf, sm, sff, smm, sfm = [boxed[i][t] for i in range(5)]
@@ -339,25 +350,33 @@
             for z, total in enumerate(windows_of_nine([coef[col, p, rows, :] for p in range(COEF_PLANES)])):
                 zcoef[col, z, rows, :] = total
 
-    def slope_plane(z):
-        summed = []
-        for col in range(9):
-            summed.append(windows_of_nine([zcoef[col, z, pl.ds(m, 8, stride=5), :] for m in range(13)]))
-        for j in range(5):
-            boxed = [box_along_x([summed[3 * i + t][j] for t in range(3)], lane) for i in range(3)]
-            centre = pl.ds(HALO + j, 8, stride=5)
-            tail = raw[4, HALO + z, centre, :]
-            f = [raw[0, HALO + z, centre, :], raw[1, HALO + z, centre, :], tail]
-            m = [raw[2, HALO + z, centre, :], raw[3, HALO + z, centre, :], pltpu.roll(tail, 64, 1)]
-            for t in range(3):
-                slope = f[t] * boxed[0][t] + m[t] * boxed[1][t] - boxed[2][t]
-                for c in range(3):
-                    weighted[c, t, j, z] = slope * grad[t, c, z, pl.ds(j, 8, stride=5), :]
+    def slope_planes(planes):
+        for s, z in enumerate(planes):
+            for col in range(9):
+                total = windows_of_nine([zcoef[col, z, pl.ds(m, 8, stride=5), :] for m in range(13)])
+                for j in range(5):
+                    stage_y[s, j, col] = total[j]
+        for s in range(2):
+            for j in range(5):
+                for i in range(3):
+                    three = three_along_x([stage_y[s, j, 3 * i + t] for t in range(3)], 1, lane)
+                    for t in range(3):
+                        stage_x[s, j, 3 * i + t] = three[t]
+        for s, z in enumerate(planes):
+            for j in range(5):
+                boxed = [three_along_x([stage_x[s, j, 3 * i + t] for t in range(3)], 3, lane) for i in range(3)]
+                centre = pl.ds(HALO + j, 8, stride=5)
+                tail = raw[4, HALO + z, centre, :]
+                f = [raw[0, HALO + z, centre, :], raw[1, HALO + z, centre, :], tail]
+                m = [raw[2, HALO + z, centre, :], raw[3, HALO + z, centre, :], pltpu.roll(tail, 64, 1)]
+                for t in range(3):
+                    slope = f[t] * boxed[0][t] + m[t] * boxed[1][t] - boxed[2][t]
+                    for c in range(3):
+                        weighted[c, t, j, z] = slope * grad[t, c, z, pl.ds(j, 8, stride=5), :]
 
     @pl.loop(0, 5)
     def _(z):
-        slope_plane(z)
-        slope_plane(z + 5)
+        slope_planes((z, z + 5))
 
     wy = [spline_weights(j) for j in range(SPACING)]
     wz = [[-2.0 * SIM_WEIGHT * w for w in ws] for ws in wy]
@@ -515,6 +534,8 @@
             pltpu.VMEM((13, COEF_PLANES, RAW_ROWS, 128), f32),
             pltpu.VMEM((2, 13, RAW_ROWS, 128), f32),
             pltpu.VMEM((26, RAW_ROWS, 128), f32),
+            pltpu.VMEM((2, 6, 15, 8, 128), f32),
+            pltpu.VMEM((2, 6, 15, 8, 128), f32),
             pltpu.VMEM((9, COEF_PLANES, COEF_ROWS, 128), f32),
             pltpu.VMEM((9, PLANES, COEF_ROWS, 128), f32),
             pltpu.VMEM((3, 3, 5, PLANES, 8, 128), f32),

time: 74.9 us -> 46.2 us (0.62)
  Pallas kernels: 73.4 us -> 44.7 us
    pallas_call x1, Pallas kernels: 73.4 us -> 44.7 us  [local_gradient(): pl.pallas_call(functools.partial(kernel, depth), out_shape=jax.ShapeDtype...]
where the time goes in v2:
time: 46.2 us; the launch traced here: 46.1 us
  Pallas kernels  44.7 us (97%)
  local copies, waits for them, and re-layouts  1.35 us (3%)
    pallas_call x1, Pallas kernels, local_gradient(): pl.pallas_call(functools.partial(kernel, depth), out_shape=jax.ShapeDtype...  44.7 us
    unnamed x1, local copies, waits for them, and re-layouts  1.35 us

profile of v2, /device:TPU:24, one launch (start us, length us, event | category | flops | bytes accessed | tf_op | source)
XLA Modules:
  0.0 46.1 jit_solution(10686593917562660813)
XLA Ops:
  0.0 44.7 %shard_map.55 = f32[2,3,8,64]{3,2,1,0:T(8,128)} custom-call(f32[10,40,320]{2,1,0:T(8,128)} %f_hbm.1, f32[10,40,320]{2,1,0:T(8,128)} %m_hbm.1, f32[3,10,40,320]{3,2,1,0:T(8,128)} %g_hbm.1, bf16[384,128]{1,0:T(8,128)(2,1)} %constant.4.clone.bh_hbm, bf16[384,128]{1,0:T(8,128)(2,1)} %constant.5.clone.bl_hbm), custom_call_target="tpu_custom_call" | custom-call | tf_op jit(solution)/shard_map/pallas_call | solution.py:521
  44.7 1.3 %copy.7 = f32[2,3,8,64]{3,2,1,0:T(8,128)} copy(f32[2,3,8,64]{3,2,1,0:T(8,128)} %shard_map.55) | data formatting | bytes 24576

commit v3 on v2

--- a/solution.py
+++ b/solution.py
@@ -25,6 +25,7 @@
 COEF_PLANES = PLANES + 2 * RADIUS
 COEF_ROWS = ROWS + 2 * RADIUS
 PAIRS = (0, 8, 2, 6, 4)
+UPFRONT = 2
 
 
 def spline_weights(step):
@@ -99,8 +100,8 @@
 def kernel(
     depth, f_hbm, m_hbm, g_hbm, bh_hbm, bl_hbm, out_ref,
     raw, f_tail, m_tail, grad, g_tail, bh, bl, own_sum, halo_sum, zsum, stage_y, stage_x, coef, zcoef, weighted, wide,
-    sums, from_next, from_prev, from_side, from_next_side, from_prev_side,
-    local_sem, y_send, y_recv, z_send, z_recv, s_send, s_recv, e_send, e_recv,
+    sums, passing, from_next, from_prev, from_side, from_next_side, from_prev_side,
+    local_sem, y_send, y_recv, z_send, z_recv, s_send, s_recv, hop_send, hop_recv, e_send, e_recv,
 ):
     gz = lax.axis_index("gz")
     gy = lax.axis_index("gy")
@@ -112,6 +113,10 @@
     before_side = (jnp.maximum(gz - 1, 0), other)
     after_side = (jnp.minimum(gz + 1, depth - 1), other)
     side = (gz, other)
+    middle = depth // 2
+    detour = depth >= 4
+    is_low_mid = (gz == middle - 1) if detour else (gz < 0)
+    is_high_mid = (gz == middle) if detour else (gz < 0)
 
     local = []
 
@@ -146,6 +151,17 @@
         pl.semaphore_signal(barrier, inc=1, device_id=after, device_id_type=MESH)
         pl.semaphore_signal(barrier, inc=1, device_id=after_side, device_id_type=MESH)
 
+    if detour:
+        @pl.when(is_low_mid | is_high_mid)
+        def _():
+            for far_slab in (0, depth - 1):
+                pl.semaphore_signal(barrier, inc=1, device_id=(far_slab, gy), device_id_type=MESH)
+
+        @pl.when(is_first | is_last)
+        def _():
+            for far_slab in (middle - 1, middle):
+                pl.semaphore_signal(barrier, inc=1, device_id=(far_slab, gy), device_id_type=MESH)
+
     lane = lax.broadcasted_iota(jnp.int32, (8, 128), 1)
     row = lax.broadcasted_iota(jnp.int32, (8, 128), 0)
     zero = jnp.zeros((8, 128), jnp.float32)
@@ -163,13 +179,22 @@
     for copy in local[2:6]:
         copy.wait()
 
-    @pl.when(is_first | is_last)
-    def _():
-        pl.semaphore_wait(barrier, 3)
-
-    @pl.when(jnp.logical_not(is_first | is_last))
-    def _():
-        pl.semaphore_wait(barrier, 5)
+    if detour:
+        @pl.when(is_low_mid | is_high_mid)
+        def _():
+            pl.semaphore_wait(barrier, 7)
+
+        @pl.when(jnp.logical_not(is_low_mid | is_high_mid))
+        def _():
+            pl.semaphore_wait(barrier, 5)
+    else:
+        @pl.when(is_first | is_last)
+        def _():
+            pl.semaphore_wait(barrier, 3)
+
+        @pl.when(jnp.logical_not(is_first | is_last))
+        def _():
+            pl.semaphore_wait(barrier, 5)
 
     src_row = pl.multiple_of(40 - 32 * gy, 8)
     y_copies = []
@@ -182,51 +207,132 @@
         copy.start()
         y_copies.append(copy)
 
-    def to_after(k, rows, send, recv):
-        return pltpu.make_async_remote_copy(
-            src_ref=raw.at[:, pl.ds(16 - 2 * k, 2), rows, :],
-            dst_ref=raw.at[:, pl.ds(6 - 2 * k, 2), rows, :],
-            send_sem=send.at[0, k], recv_sem=recv.at[0, k], device_id=after, device_id_type=MESH,
-        )
-
-    def to_before(k, rows, send, recv):
-        return pltpu.make_async_remote_copy(
-            src_ref=raw.at[:, pl.ds(8 + 2 * k, 2), rows, :],
-            dst_ref=raw.at[:, pl.ds(18 + 2 * k, 2), rows, :],
-            send_sem=send.at[1, k], recv_sem=recv.at[1, k], device_id=before, device_id_type=MESH,
+    def plane_to_after(k, h):
+        return pltpu.make_async_remote_copy(
+            src_ref=raw.at[:, 17 - 2 * k - h, rows_own, :],
+            dst_ref=raw.at[:, 7 - 2 * k - h, rows_own, :],
+            send_sem=z_send.at[0, k, h], recv_sem=z_recv.at[0, k, h], device_id=after, device_id_type=MESH,
+        )
+
+    def plane_to_before(k, h):
+        return pltpu.make_async_remote_copy(
+            src_ref=raw.at[:, 8 + 2 * k + h, rows_own, :],
+            dst_ref=raw.at[:, 18 + 2 * k + h, rows_own, :],
+            send_sem=z_send.at[1, k, h], recv_sem=z_recv.at[1, k, h], device_id=before, device_id_type=MESH,
         )
 
     strip = pl.ds(strip_row, 8)
 
-    def start_planes(k, rows, send, recv):
-        @pl.when(jnp.logical_not(is_last))
-        def _():
-            to_after(k, rows, send, recv).start()
-
-        @pl.when(jnp.logical_not(is_first))
-        def _():
-            to_before(k, rows, send, recv).start()
-
-    def wait_planes(k, rows, send, recv):
-        @pl.when(jnp.logical_not(is_first))
-        def _():
-            to_after(k, rows, send, recv).wait_recv()
-
-        @pl.when(jnp.logical_not(is_last))
-        def _():
-            to_before(k, rows, send, recv).wait_recv()
-
-    def wait_sent(k, rows, send, recv):
-        @pl.when(jnp.logical_not(is_last))
-        def _():
-            to_after(k, rows, send, recv).wait_send()
-
-        @pl.when(jnp.logical_not(is_first))
-        def _():
-            to_before(k, rows, send, recv).wait_send()
-
-    for k in range(3):
-        start_planes(k, rows_own, z_send, z_recv)
+    def strip_to_after(k):
+        return pltpu.make_async_remote_copy(
+            src_ref=raw.at[:, pl.ds(16 - 2 * k, 2), strip, :],
+            dst_ref=raw.at[:, pl.ds(6 - 2 * k, 2), strip, :],
+            send_sem=s_send.at[0, k], recv_sem=s_recv.at[0, k], device_id=after, device_id_type=MESH,
+        )
+
+    def strip_to_before(k):
+        return pltpu.make_async_remote_copy(
+            src_ref=raw.at[:, pl.ds(8 + 2 * k, 2), strip, :],
+            dst_ref=raw.at[:, pl.ds(18 + 2 * k, 2), strip, :],
+            send_sem=s_send.at[1, k], recv_sem=s_recv.at[1, k], device_id=before, device_id_type=MESH,
+        )
+
+    def hop_up(k):
+        return pltpu.make_async_remote_copy(
+            src_ref=raw.at[:, 16 - 2 * k, rows_own, :], dst_ref=passing.at[k],
+            send_sem=z_send.at[0, k, 1], recv_sem=hop_recv.at[k], device_id=(depth - 1, gy), device_id_type=MESH,
+        )
+
+    def hop_down(k):
+        return pltpu.make_async_remote_copy(
+            src_ref=raw.at[:, 9 + 2 * k, rows_own, :], dst_ref=passing.at[k],
+            send_sem=z_send.at[1, k, 1], recv_sem=hop_recv.at[k], device_id=(0, gy), device_id_type=MESH,
+        )
+
+    def on_up(k):
+        return pltpu.make_async_remote_copy(
+            src_ref=passing.at[k], dst_ref=raw.at[:, 6 - 2 * k, rows_own, :],
+            send_sem=hop_send.at[k], recv_sem=z_recv.at[0, k, 1], device_id=(middle, gy), device_id_type=MESH,
+        )
+
+    def on_down(k):
+        return pltpu.make_async_remote_copy(
+            src_ref=passing.at[k], dst_ref=raw.at[:, 19 + 2 * k, rows_own, :],
+            send_sem=hop_send.at[k], recv_sem=z_recv.at[1, k, 1], device_id=(middle - 1, gy), device_id_type=MESH,
+        )
+
+    sends_up = jnp.logical_not(is_last)
+    sends_down = jnp.logical_not(is_first)
+
+    def start_planes(k):
+        @pl.when(sends_up)
+        def _():
+            plane_to_after(k, 0).start()
+
+        @pl.when(sends_down)
+        def _():
+            plane_to_before(k, 0).start()
+
+        @pl.when(sends_up & jnp.logical_not(is_low_mid))
+        def _():
+            plane_to_after(k, 1).start()
+
+        @pl.when(sends_down & jnp.logical_not(is_high_mid))
+        def _():
+            plane_to_before(k, 1).start()
+
+    def start_strips(k):
+        @pl.when(sends_up)
+        def _():
+            strip_to_after(k).start()
+
+        @pl.when(sends_down)
+        def _():
+            strip_to_before(k).start()
+
+    def pass_on(k):
+        if detour:
+            @pl.when(is_last)
+            def _():
+                hop_up(k).wait_recv()
+                on_up(k).start()
+
+            @pl.when(is_first)
+            def _():
+                hop_down(k).wait_recv()
+                on_down(k).start()
+
+    def wait_planes(k, h):
+        @pl.when(sends_down)
+        def _():
+            plane_to_after(k, h).wait_recv()
+
+        @pl.when(sends_up)
+        def _():
+            plane_to_before(k, h).wait_recv()
+
+    def wait_strips(k):
+        @pl.when(sends_down)
+        def _():
+            strip_to_after(k).wait_recv()
+
+        @pl.when(sends_up)
+        def _():
+            strip_to_before(k).wait_recv()
+
+    if detour:
+        @pl.when(is_low_mid)
+        def _():
+            for k in range(4):
+                hop_up(k).start()
+
+        @pl.when(is_high_mid)
+        def _():
+            for k in range(4):
+                hop_down(k).start()
+
+    for k in range(UPFRONT):
+        start_planes(k)
 
     @pl.when(is_first)
     def _():
@@ -260,14 +366,19 @@
 
     y_copies[0].wait_recv()
     y_copies[1].wait_recv()
-    start_planes(0, strip, s_send, s_recv)
-    start_planes(3, rows_own, z_send, z_recv)
+    start_strips(0)
+    start_planes(UPFRONT)
+    pass_on(0)
     y_copies[2].wait_recv()
     y_copies[3].wait_recv()
-    start_planes(1, strip, s_send, s_recv)
+    start_strips(1)
+    for k in range(UPFRONT + 1, 4):
+        start_planes(k)
     y_copies[4].wait_recv()
-    start_planes(2, strip, s_send, s_recv)
-    start_planes(3, strip, s_send, s_recv)
+    start_strips(2)
+    start_strips(3)
+    for k in range(1, 4):
+        pass_on(k)
     own_windows(strip)
 
     row_valid = []
@@ -331,12 +442,12 @@
 
     @pl.loop(0, 4)
     def _(k):
-        wait_planes(k, rows_own, z_send, z_recv)
-        wait_planes(k, strip, s_send, s_recv)
+        wait_strips(k)
 
         @pl.loop(0, 2)
-        def _(half):
-            step = 2 * k + half
+        def _(h):
+            wait_planes(k, h)
+            step = 2 * k + h
             coefficients((7 - step, 10 + step), (7 - step, 18 + step))
 
     for copy in local[6:]:
@@ -496,8 +607,22 @@
     for copy in y_copies:
         copy.wait_send()
     for k in range(4):
-        wait_sent(k, rows_own, z_send, z_recv)
-        wait_sent(k, strip, s_send, s_recv)
+        @pl.when(sends_up)
+        def _():
+            plane_to_after(k, 0).wait_send()
+            plane_to_after(k, 1).wait_send()
+            strip_to_after(k).wait_send()
+
+        @pl.when(sends_down)
+        def _():
+            plane_to_before(k, 0).wait_send()
+            plane_to_before(k, 1).wait_send()
+            strip_to_before(k).wait_send()
+
+        if detour:
+            @pl.when(is_first | is_last)
+            def _():
+                on_up(k).wait_send()
     side_copy.wait_send()
 
     @pl.when(jnp.logical_not(is_first))
@@ -541,6 +666,7 @@
             pltpu.VMEM((3, 3, 5, PLANES, 8, 128), f32),
             pltpu.VMEM((240, 384), f32),
             pltpu.VMEM((5, 2, 3, 8, 128), f32),
+            pltpu.VMEM((4, 5, ROWS, 128), f32),
             pltpu.VMEM((3, 8, 128), f32),
             pltpu.VMEM((2, 3, 8, 128), f32),
             pltpu.VMEM((2, 3, 8, 128), f32),
@@ -549,10 +675,12 @@
             dma((11,)),
             dma((5,)),
             dma((5,)),
+            dma((2, 4, 2)),
+            dma((2, 4, 2)),
             dma((2, 4)),
             dma((2, 4)),
-            dma((2, 4)),
-            dma((2, 4)),
+            dma((4,)),
+            dma((4,)),
             dma((5,)),
             dma((5,)),
         ],

time: 46.2 us -> 41 us (0.89)
  Pallas kernels: 44.7 us -> 39.5 us
    pallas_call x1, Pallas kernels: 44.7 us -> 39.5 us  [local_gradient(): pl.pallas_call(functools.partial(kernel, depth), out_shape=jax.ShapeDtype...]
where the time goes in v3:
time: 41 us; the launch traced here: 40.8 us
  Pallas kernels  39.5 us (96%)
  local copies, waits for them, and re-layouts  1.35 us (3%)
    pallas_call x1, Pallas kernels, local_gradient(): pl.pallas_call(functools.partial(kernel, depth), out_shape=jax.ShapeDtype...  39.5 us
    unnamed x1, local copies, waits for them, and re-layouts  1.35 us

profile of v3, /device:TPU:24, one launch (start us, length us, event | category | flops | bytes accessed | tf_op | source)
XLA Modules:
  0.0 40.8 jit_solution(3119810231865961267)
XLA Ops:
  0.0 39.5 %shard_map.55 = f32[2,3,8,64]{3,2,1,0:T(8,128)} custom-call(f32[10,40,320]{2,1,0:T(8,128)} %f_hbm.1, f32[10,40,320]{2,1,0:T(8,128)} %m_hbm.1, f32[3,10,40,320]{3,2,1,0:T(8,128)} %g_hbm.1, bf16[384,128]{1,0:T(8,128)(2,1)} %constant.4.clone.bh_hbm, bf16[384,128]{1,0:T(8,128)(2,1)} %constant.5.clone.bl_hbm), custom_call_target="tpu_custom_call" | custom-call | tf_op jit(solution)/shard_map/pallas_call | solution.py:646
  39.5 1.3 %copy.7 = f32[2,3,8,64]{3,2,1,0:T(8,128)} copy(f32[2,3,8,64]{3,2,1,0:T(8,128)} %shard_map.55) | data formatting | bytes 24576

commit v4 on v3

--- a/solution.py
+++ b/solution.py
@@ -25,7 +25,7 @@
 COEF_PLANES = PLANES + 2 * RADIUS
 COEF_ROWS = ROWS + 2 * RADIUS
 PAIRS = (0, 8, 2, 6, 4)
-UPFRONT = 2
+DETOUR = ((2, 1), (3, 1))
 
 
 def spline_weights(step):
@@ -99,7 +99,7 @@
 
 def kernel(
     depth, f_hbm, m_hbm, g_hbm, bh_hbm, bl_hbm, out_ref,
-    raw, f_tail, m_tail, grad, g_tail, bh, bl, own_sum, halo_sum, zsum, stage_y, stage_x, coef, zcoef, weighted, wide,
+    raw, f_tail, m_tail, grad, g_tail, bh, bl, own_sum, halo_sum, zsum, ysum, stage_y, stage_x, coef, weighted, inner_sum, wide,
     sums, passing, from_next, from_prev, from_side, from_next_side, from_prev_side,
     local_sem, y_send, y_recv, z_send, z_recv, s_send, s_recv, hop_send, hop_recv, e_send, e_recv,
 ):
@@ -114,7 +114,7 @@
     after_side = (jnp.minimum(gz + 1, depth - 1), other)
     side = (gz, other)
     middle = depth // 2
-    detour = depth >= 4
+    detour = depth >= 4 and len(DETOUR) > 0
     is_low_mid = (gz == middle - 1) if detour else (gz < 0)
     is_high_mid = (gz == middle) if detour else (gz < 0)
 
@@ -169,8 +169,10 @@
 
     zero_row = pl.multiple_of(48 * gy, 8)
     strip_row = pl.multiple_of(48 - 48 * gy, 8)
-    zsum[:, pl.ds(zero_row, 8), :] = jnp.zeros((26, 8, 128), jnp.float32)
+    raw[:, :, pl.ds(zero_row, 8), :] = jnp.zeros((5, RAW_PLANES, 8, 128), jnp.float32)
     halo_sum[...] = jnp.zeros_like(halo_sum)
+    main_row = pl.multiple_of(8 * gy, 8)
+    edge_row = pl.multiple_of(40 - 40 * gy, 8)
 
     local[0].wait()
     local[1].wait()
@@ -237,49 +239,49 @@
             send_sem=s_send.at[1, k], recv_sem=s_recv.at[1, k], device_id=before, device_id_type=MESH,
         )
 
-    def hop_up(k):
+    def hop_up(i):
+        k, h = DETOUR[i]
         return pltpu.make_async_remote_copy(
-            src_ref=raw.at[:, 16 - 2 * k, rows_own, :], dst_ref=passing.at[k],
-            send_sem=z_send.at[0, k, 1], recv_sem=hop_recv.at[k], device_id=(depth - 1, gy), device_id_type=MESH,
-        )
-
-    def hop_down(k):
+            src_ref=raw.at[:, 17 - 2 * k - h, rows_own, :], dst_ref=passing.at[i],
+            send_sem=z_send.at[0, k, h], recv_sem=hop_recv.at[i], device_id=(depth - 1, gy), device_id_type=MESH,
+        )
+
+    def hop_down(i):
+        k, h = DETOUR[i]
         return pltpu.make_async_remote_copy(
-            src_ref=raw.at[:, 9 + 2 * k, rows_own, :], dst_ref=passing.at[k],
-            send_sem=z_send.at[1, k, 1], recv_sem=hop_recv.at[k], device_id=(0, gy), device_id_type=MESH,
-        )
-
-    def on_up(k):
+            src_ref=raw.at[:, 8 + 2 * k + h, rows_own, :], dst_ref=passing.at[i],
+            send_sem=z_send.at[1, k, h], recv_sem=hop_recv.at[i], device_id=(0, gy), device_id_type=MESH,
+        )
+
+    def on_up(i):
+        k, h = DETOUR[i]
         return pltpu.make_async_remote_copy(
-            src_ref=passing.at[k], dst_ref=raw.at[:, 6 - 2 * k, rows_own, :],
-            send_sem=hop_send.at[k], recv_sem=z_recv.at[0, k, 1], device_id=(middle, gy), device_id_type=MESH,
-        )
-
-    def on_down(k):
+            src_ref=passing.at[i], dst_ref=raw.at[:, 7 - 2 * k - h, rows_own, :],
+            send_sem=hop_send.at[i], recv_sem=z_recv.at[0, k, h], device_id=(middle, gy), device_id_type=MESH,
+        )
+
+    def on_down(i):
+        k, h = DETOUR[i]
         return pltpu.make_async_remote_copy(
-            src_ref=passing.at[k], dst_ref=raw.at[:, 19 + 2 * k, rows_own, :],
-            send_sem=hop_send.at[k], recv_sem=z_recv.at[1, k, 1], device_id=(middle - 1, gy), device_id_type=MESH,
+            src_ref=passing.at[i], dst_ref=raw.at[:, 18 + 2 * k + h, rows_own, :],
+            send_sem=hop_send.at[i], recv_sem=z_recv.at[1, k, h], device_id=(middle - 1, gy), device_id_type=MESH,
         )
 
     sends_up = jnp.logical_not(is_last)
     sends_down = jnp.logical_not(is_first)
 
-    def start_planes(k):
-        @pl.when(sends_up)
-        def _():
-            plane_to_after(k, 0).start()
-
-        @pl.when(sends_down)
-        def _():
-            plane_to_before(k, 0).start()
-
-        @pl.when(sends_up & jnp.logical_not(is_low_mid))
-        def _():
-            plane_to_after(k, 1).start()
-
-        @pl.when(sends_down & jnp.logical_not(is_high_mid))
-        def _():
-            plane_to_before(k, 1).start()
+    def start_plane(k, h):
+        goes_round = (k, h) in DETOUR
+        up = sends_up & jnp.logical_not(is_low_mid) if goes_round else sends_up
+        down = sends_down & jnp.logical_not(is_high_mid) if goes_round else sends_down
+
+        @pl.when(up)
+        def _():
+            plane_to_after(k, h).start()
+
+        @pl.when(down)
+        def _():
+            plane_to_before(k, h).start()
 
     def start_strips(k):
         @pl.when(sends_up)
@@ -290,17 +292,17 @@
         def _():
             strip_to_before(k).start()
 
-    def pass_on(k):
-        if detour:
+    def pass_on(i):
+        if detour and i < len(DETOUR):
             @pl.when(is_last)
             def _():
-                hop_up(k).wait_recv()
-                on_up(k).start()
+                hop_up(i).wait_recv()
+                on_up(i).start()
 
             @pl.when(is_first)
             def _():
-                hop_down(k).wait_recv()
-                on_down(k).start()
+                hop_down(i).wait_recv()
+                on_down(i).start()
 
     def wait_planes(k, h):
         @pl.when(sends_down)
@@ -323,16 +325,16 @@
     if detour:
         @pl.when(is_low_mid)
         def _():
-            for k in range(4):
-                hop_up(k).start()
+            for i in range(len(DETOUR)):
+                hop_up(i).start()
 
         @pl.when(is_high_mid)
         def _():
-            for k in range(4):
-                hop_down(k).start()
-
-    for k in range(UPFRONT):
-        start_planes(k)
+            for i in range(len(DETOUR)):
+                hop_down(i).start()
+
+    for k, h in ((0, 0), (0, 1), (1, 0), (1, 1), (2, 0)):
+        start_plane(k, h)
 
     @pl.when(is_first)
     def _():
@@ -360,69 +362,58 @@
             for p, total in enumerate(suffix_sums(values[1:])):
                 own_sum[col, 9 + p, rows, :] = total
 
-    @pl.loop(0, 5)
+    @pl.loop(0, 6)
     def _(i):
-        own_windows(pl.ds(pl.multiple_of(8 + 8 * i, 8), 8))
-
-    y_copies[0].wait_recv()
-    y_copies[1].wait_recv()
-    start_strips(0)
-    start_planes(UPFRONT)
-    pass_on(0)
-    y_copies[2].wait_recv()
-    y_copies[3].wait_recv()
-    start_strips(1)
-    for k in range(UPFRONT + 1, 4):
-        start_planes(k)
-    y_copies[4].wait_recv()
-    start_strips(2)
-    start_strips(3)
-    for k in range(1, 4):
-        pass_on(k)
-    own_windows(strip)
-
-    row_valid = []
-    for j in range(6):
-        position = 6 * row + j + 40 * gy - 4
-        row_valid.append(jnp.where((position >= 0) & (position < 80), 1.0, 0.0))
-
-    groups = [pl.ds(8 + 8 * i, 8) for i in range(5)] + [strip]
-
-    def coefficients(planes, halo):
-        for s in range(2):
-            for rows in groups:
+        own_windows(pl.ds(pl.multiple_of(main_row + 8 * i, 8), 8))
+
+    def coefficients(items, base, count, part):
+        offset = 48 * part
+        for n, (plane, halo, side_of) in enumerate(items):
+            for g in range(count + 1):
+                rows = pl.ds(pl.multiple_of(base + 8 * g, 8), 8)
+                here = pl.ds(8 * g, 8)
                 if halo is None:
                     for col in range(13):
-                        zsum[13 * s + col, rows, :] = own_sum[col, planes[s], rows, :]
+                        zsum[13 * n + col, here, :] = own_sum[col, plane, rows, :]
                 else:
-                    fields = fields_of(halo[s], rows)
+                    there = pl.ds(offset + 8 * g, 8)
+                    fields = fields_of(halo, rows)
                     for col in range(13):
-                        total = halo_sum[s, col, rows, :] + fields[col]
-                        halo_sum[s, col, rows, :] = total
-                        zsum[13 * s + col, rows, :] = total + own_sum[col, planes[s], rows, :]
-        for s in range(2):
+                        total = halo_sum[side_of, col, there, :] + fields[col]
+                        halo_sum[side_of, col, there, :] = total
+                        zsum[13 * n + col, here, :] = total + own_sum[col, plane, rows, :]
+        for n in range(len(items)):
             for col in range(13):
-                total = windows_of_nine([zsum[13 * s + col, pl.ds(m, 8, stride=6), :] for m in range(14)])
-                for j in range(6):
+                at = 13 * n + col
+                for g in range(count + 1):
+                    ysum[at, pl.ds(8 * g, 8), :] = (
+                        zsum[at, pl.ds(8 * g, 8), :] + zsum[at, pl.ds(8 * g + 1, 8), :] + zsum[at, pl.ds(8 * g + 2, 8), :]
+                    )
+                for j in range(count):
+                    total = (
+                        ysum[at, pl.ds(8 * j, 8), :] + ysum[at, pl.ds(8 * j + 3, 8), :] + ysum[at, pl.ds(8 * j + 6, 8), :]
+                    )
                     if col < 10:
-                        stage_y[s, j, 3 * (col % 5) + col // 5] = total[j]
+                        stage_y[n, j, 3 * (col % 5) + col // 5] = total
                     elif col == 12:
-                        stage_y[s, j, 14] = jnp.where(low_half, total[j], 0.0)
+                        stage_y[n, j, 14] = jnp.where(low_half, total, 0.0)
                     else:
-                        stage_y[s, j, 6 * (col - 10) + 2] = jnp.where(low_half, total[j], 0.0)
-                        stage_y[s, j, 6 * (col - 10) + 5] = jnp.where(low_half, pltpu.roll(total[j], 64, 1), 0.0)
-        for s in range(2):
-            for j in range(6):
+                        stage_y[n, j, 6 * (col - 10) + 2] = jnp.where(low_half, total, 0.0)
+                        stage_y[n, j, 6 * (col - 10) + 5] = jnp.where(low_half, pltpu.roll(total, 64, 1), 0.0)
+        for n in range(len(items)):
+            for j in range(count):
                 for i in range(5):
-                    three = three_along_x([stage_y[s, j, 3 * i + t] for t in range(3)], 1, lane)
+                    three = three_along_x([stage_y[n, j, 3 * i + t] for t in range(3)], 1, lane)
                     for t in range(3):
-                        stage_x[s, j, 3 * i + t] = three[t]
-        for s in range(2):
-            position = gz * PLANES + planes[s] - RADIUS
-            inside = jnp.where((position >= 0) & (position < depth * PLANES), 1.0, 0.0)
-            for j in range(6):
-                boxed = [three_along_x([stage_x[s, j, 3 * i + t] for t in range(3)], 3, lane) for i in range(5)]
-                valid = row_valid[j] * inside
+                        stage_x[n, j, 3 * i + t] = three[t]
+        for n, (plane, halo, side_of) in enumerate(items):
+            position = gz * PLANES + plane - RADIUS
+            inside = (position >= 0) & (position < depth * PLANES)
+            for j in range(count):
+                boxed = [three_along_x([stage_x[n, j, 3 * i + t] for t in range(3)], 3, lane) for i in range(5)]
+                position = base + 8 * j + row + 40 * gy - RADIUS
+                valid = jnp.where(inside & (position >= 0) & (position < 80), 1.0, 0.0)
+                where = pl.ds(pl.multiple_of(base + 8 * j, 8), 8)
                 for t in range(3):
                     sf, sm, sff, smm, sfm = [boxed[i][t] for i in range(5)]
                     mf = sf * (1.0 / WINDOW)
@@ -433,38 +424,33 @@
                     r = 1.0 / (p * q)
                     cross = a * r
                     moving = -cross * a * (r * p)
-                    where = pl.ds(j, 8, stride=6)
-                    coef[t, planes[s], where, :] = cross
-                    coef[3 + t, planes[s], where, :] = moving
-                    coef[6 + t, planes[s], where, :] = cross * mf + moving * mm
-
-    coefficients((8, 9), None)
-
-    @pl.loop(0, 4)
-    def _(k):
-        wait_strips(k)
-
-        @pl.loop(0, 2)
-        def _(h):
-            wait_planes(k, h)
-            step = 2 * k + h
-            coefficients((7 - step, 10 + step), (7 - step, 18 + step))
-
-    for copy in local[6:]:
-        copy.wait()
-    grad[2] = jnp.concatenate([g_tail[...], jnp.zeros_like(g_tail)], axis=-1)
-
-    @pl.loop(0, 9)
-    def _(col):
-        for g in range(6):
-            rows = pl.ds(8 * g, 8)
-            for z, total in enumerate(windows_of_nine([coef[col, p, rows, :] for p in range(COEF_PLANES)])):
-                zcoef[col, z, rows, :] = total
-
-    def slope_planes(planes):
+                    for i, value in enumerate((cross, moving, cross * mf + moving * mm)):
+                        if halo is not None:
+                            value = value + coef[3 * i + t, plane + (1, -1)[side_of], where, :]
+                        coef[3 * i + t, plane, where, :] = value
+
+    middle_items = [(8, None, 0), (9, None, 1)]
+
+    def step_items(step):
+        return [(7 - step, 7 - step, 0), (10 + step, 18 + step, 1)]
+
+    def main_part(items):
+        coefficients(items, main_row, 5, 0)
+
+    def edge_part(items):
+        coefficients(items, edge_row, 1, 1)
+
+    def slope_planes(planes, ends):
         for s, z in enumerate(planes):
             for col in range(9):
-                total = windows_of_nine([zcoef[col, z, pl.ds(m, 8, stride=5), :] for m in range(13)])
+                values = []
+                for m in range(13):
+                    where = pl.ds(m, 8, stride=5)
+                    if ends:
+                        values.append(coef[col, (0, COEF_PLANES - 1)[s], where, :])
+                    else:
+                        values.append(coef[col, z, where, :] + coef[col, z + 2 * RADIUS, where, :])
+                total = windows_of_nine(values)
                 for j in range(5):
                     stage_y[s, j, col] = total[j]
         for s in range(2):
@@ -485,27 +471,94 @@
                     for c in range(3):
                         weighted[c, t, j, z] = slope * grad[t, c, z, pl.ds(j, 8, stride=5), :]
 
-    @pl.loop(0, 5)
-    def _(z):
-        slope_planes((z, z + 5))
+    main_part(middle_items)
+
+    for copy in local[6:]:
+        copy.wait()
+    grad[2] = jnp.concatenate([g_tail[...], jnp.zeros_like(g_tail)], axis=-1)
+
+    @pl.loop(0, 7)
+    def _(step):
+        wait_planes(step // 2, step % 2)
+        main_part(step_items(step))
+
+        @pl.when(step == 0)
+        def _():
+            pass_on(0)
+
+        @pl.when(step == 1)
+        def _():
+            y_copies[0].wait_recv()
+            y_copies[1].wait_recv()
+            start_strips(0)
+            start_plane(2, 1)
+            start_plane(3, 0)
+            pass_on(1)
+
+        @pl.when(step == 2)
+        def _():
+            y_copies[2].wait_recv()
+            y_copies[3].wait_recv()
+            start_strips(1)
+            pass_on(2)
+
+        @pl.when(step == 3)
+        def _():
+            y_copies[4].wait_recv()
+            start_strips(2)
+            start_strips(3)
+            start_plane(3, 1)
+            pass_on(3)
+            own_windows(strip)
+
+        @pl.when(step == 5)
+        def _():
+            wait_strips(0)
+            wait_strips(1)
+            edge_part(middle_items + step_items(0) + step_items(1) + step_items(2))
+
+    wait_strips(2)
+    wait_strips(3)
+    edge_part(step_items(3) + step_items(4) + step_items(5) + step_items(6))
+
+    @pl.loop(3, 7)
+    def _(step):
+        slope_planes((7 - step, 2 + step), False)
 
     wy = [spline_weights(j) for j in range(SPACING)]
     wz = [[-2.0 * SIM_WEIGHT * w for w in ws] for ws in wy]
+
+    def add_plane(slots, z, value):
+        for k in range(4):
+            weight = wz[z % SPACING][k]
+            if weight != 0.0:
+                m = z // SPACING + k
+                slots[m] = weight * value if slots[m] is None else slots[m] + weight * value
+
+    for t in range(3):
+        @pl.loop(0, 3)
+        def _(c):
+            for j in range(SPACING):
+                slots = [None] * 5
+                for z in range(1, PLANES - 1):
+                    add_plane(slots, z, weighted[c, t, j, z])
+                for m in range(5):
+                    inner_sum[c, t, j, m] = slots[m]
+
+    wait_planes(3, 1)
+    main_part(step_items(7))
+    edge_part(step_items(7))
+    slope_planes((0, PLANES - 1), True)
+
     for t in range(3):
         @pl.loop(0, 3)
         def _(c):
             slots = []
             for j in range(SPACING):
-                v = [weighted[c, t, j, z] for z in range(PLANES)]
-                part = []
-                for i in range(2):
-                    for k in range(4):
-                        total = wz[0][k] * v[5 * i]
-                        for step in range(1, SPACING):
-                            if wz[step][k] != 0.0:
-                                total = total + wz[step][k] * v[5 * i + step]
-                        part.append(total)
-                slots.append([part[0], part[1] + part[4], part[2] + part[5], part[3] + part[6], part[7]])
+                parts = [inner_sum[c, t, j, m] for m in range(5)]
+                add_plane(parts, 0, weighted[c, t, j, 0])
+                add_plane(parts, PLANES - 1, weighted[c, t, j, PLANES - 1])
+                slots.append(parts)
             for m in range(5):
                 y = []
                 for k in range(4):
@@ -619,7 +672,7 @@
             plane_to_before(k, 1).wait_send()
             strip_to_before(k).wait_send()
 
-        if detour:
+        if detour and k < len(DETOUR):
             @pl.when(is_first | is_last)
             def _():
                 on_up(k).wait_send()
@@ -657,13 +710,14 @@
             pltpu.VMEM((384, 128), jnp.bfloat16),
             pltpu.VMEM((384, 128), jnp.bfloat16),
             pltpu.VMEM((13, COEF_PLANES, RAW_ROWS, 128), f32),
-            pltpu.VMEM((2, 13, RAW_ROWS, 128), f32),
-            pltpu.VMEM((26, RAW_ROWS, 128), f32),
-            pltpu.VMEM((2, 6, 15, 8, 128), f32),
-            pltpu.VMEM((2, 6, 15, 8, 128), f32),
+            pltpu.VMEM((2, 13, 64, 128), f32),
+            pltpu.VMEM((104, RAW_ROWS, 128), f32),
+            pltpu.VMEM((104, RAW_ROWS, 128), f32),
+            pltpu.VMEM((8, 5, 15, 8, 128), f32),
+            pltpu.VMEM((8, 5, 15, 8, 128), f32),
             pltpu.VMEM((9, COEF_PLANES, COEF_ROWS, 128), f32),
-            pltpu.VMEM((9, PLANES, COEF_ROWS, 128), f32),
             pltpu.VMEM((3, 3, 5, PLANES, 8, 128), f32),
+            pltpu.VMEM((3, 3, 5, 5, 8, 128), f32),
             pltpu.VMEM((240, 384), f32),
             pltpu.VMEM((5, 2, 3, 8, 128), f32),
             pltpu.VMEM((4, 5, ROWS, 128), f32),
@@ -684,7 +738,7 @@
             dma((5,)),
             dma((5,)),
         ],
-        compiler_params=pltpu.CompilerParams(collective_id=0, has_side_effects=True, vmem_limit_bytes=60 * 1024 * 1024),
+        compiler_params=pltpu.CompilerParams(collective_id=0, has_side_effects=True, vmem_limit_bytes=56500000),
     )(fixed_image, moving_image, moving_grad, high, low)
 
 

time: 41 us -> 37.5 us (0.915)
  Pallas kernels: 39.5 us -> 36.8 us
  local copies, waits for them, and re-layouts: 1.35 us -> 0.61 us
    pallas_call x1, Pallas kernels: 39.5 us -> 36.8 us  [local_gradient(): pl.pallas_call(functools.partial(kernel, depth), out_shape=jax.ShapeDtype...]
    unnamed x1, local copies, waits for them, and re-layouts: 1.35 us -> 0.61 us
where the time goes in v4:
time: 37.5 us
  Pallas kernels  36.8 us (98%)
  local copies, waits for them, and re-layouts  0.61 us (2%)
    pallas_call x1, Pallas kernels, local_gradient(): pl.pallas_call(functools.partial(kernel, depth), out_shape=jax.ShapeDtype...  36.8 us

profile of v4, /device:TPU:24, one launch (start us, length us, event | category | flops | bytes accessed | tf_op | source)
XLA Modules:
  0.0 37.5 jit_solution(9766610141708403342)
XLA Ops:
  0.0 36.8 %shard_map.55 = f32[2,3,8,64]{3,2,1,0:T(8,128)S(1)} custom-call(f32[10,40,320]{2,1,0:T(8,128)} %f_hbm.1, f32[10,40,320]{2,1,0:T(8,128)} %m_hbm.1, f32[3,10,40,320]{3,2,1,0:T(8,128)} %g_hbm.1, bf16[384,128]{1,0:T(8,128)(2,1)} %constant.4.clone.bh_hbm, bf16[384,128]{1,0:T(8,128)(2,1)} %constant.5.clone.bl_hbm), custom_call_target="tpu_custom_call" | custom-call | tf_op jit(solution)/shard_map/pallas_call | solution.py:699
  36.9 0.6 %copy.7 = f32[2,3,8,64]{3,2,1,0:T(8,128)} copy(f32[2,3,8,64]{3,2,1,0:T(8,128)S(1)} %shard_map.55) | data formatting | bytes 24576

commit v5 on v4

--- a/solution.py
+++ b/solution.py
@@ -25,7 +25,9 @@
 COEF_PLANES = PLANES + 2 * RADIUS
 COEF_ROWS = ROWS + 2 * RADIUS
 PAIRS = (0, 8, 2, 6, 4)
-DETOUR = ((2, 1), (3, 1))
+DETOUR = (((2, 0), 0), ((2, 1), 0), ((3, 0), 0), ((3, 1), 0))
+PASS_AFTER = (3, 4, 5, 6)
+ROUND = tuple(plane for plane, way in DETOUR)
 
 
 def spline_weights(step):
@@ -240,28 +242,30 @@
         )
 
     def hop_up(i):
-        k, h = DETOUR[i]
+        (k, h), way = DETOUR[i]
         return pltpu.make_async_remote_copy(
             src_ref=raw.at[:, 17 - 2 * k - h, rows_own, :], dst_ref=passing.at[i],
-            send_sem=z_send.at[0, k, h], recv_sem=hop_recv.at[i], device_id=(depth - 1, gy), device_id_type=MESH,
+            send_sem=z_send.at[0, k, h], recv_sem=hop_recv.at[i],
+            device_id=((0, depth - 1)[way], gy), device_id_type=MESH,
         )
 
     def hop_down(i):
-        k, h = DETOUR[i]
+        (k, h), way = DETOUR[i]
         return pltpu.make_async_remote_copy(
             src_ref=raw.at[:, 8 + 2 * k + h, rows_own, :], dst_ref=passing.at[i],
-            send_sem=z_send.at[1, k, h], recv_sem=hop_recv.at[i], device_id=(0, gy), device_id_type=MESH,
+            send_sem=z_send.at[1, k, h], recv_sem=hop_recv.at[i],
+            device_id=((depth - 1, 0)[way], gy), device_id_type=MESH,
         )
 
     def on_up(i):
-        k, h = DETOUR[i]
+        (k, h), way = DETOUR[i]
         return pltpu.make_async_remote_copy(
             src_ref=passing.at[i], dst_ref=raw.at[:, 7 - 2 * k - h, rows_own, :],
             send_sem=hop_send.at[i], recv_sem=z_recv.at[0, k, h], device_id=(middle, gy), device_id_type=MESH,
         )
 
     def on_down(i):
-        k, h = DETOUR[i]
+        (k, h), way = DETOUR[i]
         return pltpu.make_async_remote_copy(
             src_ref=passing.at[i], dst_ref=raw.at[:, 18 + 2 * k + h, rows_own, :],
             send_sem=hop_send.at[i], recv_sem=z_recv.at[1, k, h], device_id=(middle - 1, gy), device_id_type=MESH,
@@ -271,7 +275,7 @@
     sends_down = jnp.logical_not(is_first)
 
     def start_plane(k, h):
-        goes_round = (k, h) in DETOUR
+        goes_round = (k, h) in ROUND
         up = sends_up & jnp.logical_not(is_low_mid) if goes_round else sends_up
         down = sends_down & jnp.logical_not(is_high_mid) if goes_round else sends_down
 
@@ -292,14 +296,25 @@
         def _():
             strip_to_before(k).start()
 
+    def start_hop(i):
+        @pl.when(is_low_mid)
+        def _():
+            hop_up(i).start()
+
+        @pl.when(is_high_mid)
+        def _():
+            hop_down(i).start()
+
     def pass_on(i):
         if detour and i < len(DETOUR):
-            @pl.when(is_last)
+            way = DETOUR[i][1]
+
+            @pl.when((is_first, is_last)[way])
             def _():
                 hop_up(i).wait_recv()
                 on_up(i).start()
 
-            @pl.when(is_first)
+            @pl.when((is_last, is_first)[way])
             def _():
                 hop_down(i).wait_recv()
                 on_down(i).start()
@@ -322,19 +337,11 @@
         def _():
             strip_to_before(k).wait_recv()
 
-    if detour:
-        @pl.when(is_low_mid)
-        def _():
-            for i in range(len(DETOUR)):
-                hop_up(i).start()
-
-        @pl.when(is_high_mid)
-        def _():
-            for i in range(len(DETOUR)):
-                hop_down(i).start()
-
-    for k, h in ((0, 0), (0, 1), (1, 0), (1, 1), (2, 0)):
-        start_plane(k, h)
+    for k, h in ((0, 0), (0, 1), (1, 0), (1, 1), (2, 0), (2, 1), (3, 0), (3, 1)):
+        if (k, h) < (2, 1):
+            start_plane(k, h)
+        if detour and (k, h) in ROUND:
+            start_hop(ROUND.index((k, h)))
 
     @pl.when(is_first)
     def _():
@@ -482,9 +489,12 @@
         wait_planes(step // 2, step % 2)
         main_part(step_items(step))
 
-        @pl.when(step == 0)
-        def _():
-            pass_on(0)
+        for after_step in sorted(set(PASS_AFTER)):
+            @pl.when(step == after_step)
+            def _():
+                for i, when in enumerate(PASS_AFTER):
+                    if when == after_step:
+                        pass_on(i)
 
         @pl.when(step == 1)
         def _():
@@ -493,14 +503,12 @@
             start_strips(0)
             start_plane(2, 1)
             start_plane(3, 0)
-            pass_on(1)
 
         @pl.when(step == 2)
         def _():
             y_copies[2].wait_recv()
             y_copies[3].wait_recv()
             start_strips(1)
-            pass_on(2)
 
         @pl.when(step == 3)
         def _():
@@ -508,7 +516,6 @@
             start_strips(2)
             start_strips(3)
             start_plane(3, 1)
-            pass_on(3)
             own_windows(strip)
 
         @pl.when(step == 5)
@@ -672,10 +679,12 @@
             plane_to_before(k, 1).wait_send()
             strip_to_before(k).wait_send()
 
-        if detour and k < len(DETOUR):
-            @pl.when(is_first | is_last)
-            def _():
-                on_up(k).wait_send()
+    if detour:
+        @pl.when(is_first | is_last)
+        def _():
+            for i in range(len(DETOUR)):
+                on_up(i).wait_send()
+
     side_copy.wait_send()
 
     @pl.when(jnp.logical_not(is_first))

time: 37.5 us -> 36.6 us (0.976)
  Pallas kernels: 36.8 us -> 35.8 us
    pallas_call x1, Pallas kernels: 36.8 us -> 35.8 us  [local_gradient(): pl.pallas_call(functools.partial(kernel, depth), out_shape=jax.ShapeDtype...]
where the time goes in v5:
time: 36.6 us; the launch traced here: 36.4 us
  Pallas kernels  35.8 us (98%)
  local copies, waits for them, and re-layouts  0.61 us (2%)
    pallas_call x1, Pallas kernels, local_gradient(): pl.pallas_call(functools.partial(kernel, depth), out_shape=jax.ShapeDtype...  35.8 us

profile of v5, /device:TPU:24, one launch (start us, length us, event | category | flops | bytes accessed | tf_op | source)
XLA Modules:
  0.0 36.4 jit_solution(963421033879539355)
XLA Ops:
  0.0 35.8 %shard_map.55 = f32[2,3,8,64]{3,2,1,0:T(8,128)S(1)} custom-call(f32[10,40,320]{2,1,0:T(8,128)} %f_hbm.1, f32[10,40,320]{2,1,0:T(8,128)} %m_hbm.1, f32[3,10,40,320]{3,2,1,0:T(8,128)} %g_hbm.1, bf16[384,128]{1,0:T(8,128)(2,1)} %constant.4.clone.bh_hbm, bf16[384,128]{1,0:T(8,128)(2,1)} %constant.5.clone.bl_hbm), custom_call_target="tpu_custom_call" | custom-call | tf_op jit(solution)/shard_map/pallas_call | solution.py:708
  35.8 0.6 %copy.7 = f32[2,3,8,64]{3,2,1,0:T(8,128)} copy(f32[2,3,8,64]{3,2,1,0:T(8,128)S(1)} %shard_map.55) | data formatting | bytes 24576

commit v6 on v5

--- a/solution.py
+++ b/solution.py
@@ -25,8 +25,10 @@
 COEF_PLANES = PLANES + 2 * RADIUS
 COEF_ROWS = ROWS + 2 * RADIUS
 PAIRS = (0, 8, 2, 6, 4)
-DETOUR = (((2, 0), 0), ((2, 1), 0), ((3, 0), 0), ((3, 1), 0))
-PASS_AFTER = (3, 4, 5, 6)
+DETOUR = (((2, 1), 1), ((3, 0), 0), ((3, 1), 0))
+PASS_AFTER = (4, 5, 6)
+RELAY_AFTER = (2, 3, 4)
+LATER = ((), ((3, 1),), ())
 ROUND = tuple(plane for plane, way in DETOUR)
 
 
@@ -338,7 +340,7 @@
             strip_to_before(k).wait_recv()
 
     for k, h in ((0, 0), (0, 1), (1, 0), (1, 1), (2, 0), (2, 1), (3, 0), (3, 1)):
-        if (k, h) < (2, 1):
+        if (k, h) < (3, 1):
             start_plane(k, h)
         if detour and (k, h) in ROUND:
             start_hop(ROUND.index((k, h)))
@@ -373,9 +375,9 @@
     def _(i):
         own_windows(pl.ds(pl.multiple_of(main_row + 8 * i, 8), 8))
 
-    def coefficients(items, base, count, part):
+    def coefficients(items, base, count, part, first=0):
         offset = 48 * part
-        for n, (plane, halo, side_of) in enumerate(items):
+        for n, (plane, halo, side_of) in enumerate(items, first):
             for g in range(count + 1):
                 rows = pl.ds(pl.multiple_of(base + 8 * g, 8), 8)
                 here = pl.ds(8 * g, 8)
@@ -389,7 +391,7 @@
                         total = halo_sum[side_of, col, there, :] + fields[col]
                         halo_sum[side_of, col, there, :] = total
                         zsum[13 * n + col, here, :] = total + own_sum[col, plane, rows, :]
-        for n in range(len(items)):
+        for n in range(first, first + len(items)):
             for col in range(13):
                 at = 13 * n + col
                 for g in range(count + 1):
@@ -407,13 +409,13 @@
                     else:
                         stage_y[n, j, 6 * (col - 10) + 2] = jnp.where(low_half, total, 0.0)
                         stage_y[n, j, 6 * (col - 10) + 5] = jnp.where(low_half, pltpu.roll(total, 64, 1), 0.0)
-        for n in range(len(items)):
+        for n in range(first, first + len(items)):
             for j in range(count):
                 for i in range(5):
                     three = three_along_x([stage_y[n, j, 3 * i + t] for t in range(3)], 1, lane)
                     for t in range(3):
                         stage_x[n, j, 3 * i + t] = three[t]
-        for n, (plane, halo, side_of) in enumerate(items):
+        for n, (plane, halo, side_of) in enumerate(items, first):
             position = gz * PLANES + plane - RADIUS
             inside = (position >= 0) & (position < depth * PLANES)
             for j in range(count):
@@ -444,8 +446,8 @@
     def main_part(items):
         coefficients(items, main_row, 5, 0)
 
-    def edge_part(items):
-        coefficients(items, edge_row, 1, 1)
+    def edge_part(items, first=0):
+        coefficients(items, edge_row, 1, 1, first)
 
     def slope_planes(planes, ends):
         for s, z in enumerate(planes):
@@ -484,6 +486,22 @@
         copy.wait()
     grad[2] = jnp.concatenate([g_tail[...], jnp.zeros_like(g_tail)], axis=-1)
 
+    def relay(part):
+        if part < 2:
+            y_copies[2 * part].wait_recv()
+            y_copies[2 * part + 1].wait_recv()
+        else:
+            y_copies[4].wait_recv()
+        for k in ((0,), (1,), (2, 3))[part]:
+            start_strips(k)
+        for k, h in LATER[part]:
+            start_plane(k, h)
+
+    @pl.when(is_low_mid | is_high_mid)
+    def _():
+        for part in range(3):
+            relay(part)
+
     @pl.loop(0, 7)
     def _(step):
         wait_planes(step // 2, step % 2)
@@ -496,26 +514,13 @@
                     if when == after_step:
                         pass_on(i)
 
-        @pl.when(step == 1)
-        def _():
-            y_copies[0].wait_recv()
-            y_copies[1].wait_recv()
-            start_strips(0)
-            start_plane(2, 1)
-            start_plane(3, 0)
-
-        @pl.when(step == 2)
-        def _():
-            y_copies[2].wait_recv()
-            y_copies[3].wait_recv()
-            start_strips(1)
-
-        @pl.when(step == 3)
-        def _():
-            y_copies[4].wait_recv()
-            start_strips(2)
-            start_strips(3)
-            start_plane(3, 1)
+        for part in range(3):
+            @pl.when((step == RELAY_AFTER[part]) & jnp.logical_not(is_low_mid | is_high_mid))
+            def _():
+                relay(part)
+
+        @pl.when(step == RELAY_AFTER[2])
+        def _():
             own_windows(strip)
 
         @pl.when(step == 5)
@@ -554,7 +559,7 @@
 
     wait_planes(3, 1)
     main_part(step_items(7))
-    edge_part(step_items(7))
+    edge_part(step_items(7), 2)
     slope_planes((0, PLANES - 1), True)
 
     for t in range(3):

time: 36.6 us -> 36.1 us (0.986)
  Pallas kernels: 35.8 us -> 35.4 us
    pallas_call x1, Pallas kernels: 35.8 us -> 35.4 us  [local_gradient(): pl.pallas_call(functools.partial(kernel, depth), out_shape=jax.ShapeDtype...]
where the time goes in v6:
time: 36.1 us; the launch traced here: 36 us
  Pallas kernels  35.4 us (98%)
  local copies, waits for them, and re-layouts  0.61 us (2%)
    pallas_call x1, Pallas kernels, local_gradient(): pl.pallas_call(functools.partial(kernel, depth), out_shape=jax.ShapeDtype...  35.4 us

profile of v6, /device:TPU:24, one launch (start us, length us, event | category | flops | bytes accessed | tf_op | source)
XLA Modules:
  0.0 36.0 jit_solution(5351312710404581742)
XLA Ops:
  0.0 35.4 %shard_map.55 = f32[2,3,8,64]{3,2,1,0:T(8,128)S(1)} custom-call(f32[10,40,320]{2,1,0:T(8,128)} %f_hbm.1, f32[10,40,320]{2,1,0:T(8,128)} %m_hbm.1, f32[3,10,40,320]{3,2,1,0:T(8,128)} %g_hbm.1, bf16[384,128]{1,0:T(8,128)(2,1)} %constant.4.clone.bh_hbm, bf16[384,128]{1,0:T(8,128)(2,1)} %constant.5.clone.bl_hbm), custom_call_target="tpu_custom_call" | custom-call | tf_op jit(solution)/shard_map/pallas_call | solution.py:713
  35.4 0.6 %copy.7 = f32[2,3,8,64]{3,2,1,0:T(8,128)} copy(f32[2,3,8,64]{3,2,1,0:T(8,128)S(1)} %shard_map.55) | data formatting | bytes 24576

commit v7 on v6

--- a/solution.py
+++ b/solution.py
@@ -26,7 +26,7 @@
 COEF_ROWS = ROWS + 2 * RADIUS
 PAIRS = (0, 8, 2, 6, 4)
 DETOUR = (((2, 1), 1), ((3, 0), 0), ((3, 1), 0))
-PASS_AFTER = (4, 5, 6)
+PASS_AFTER = (3, 4, 5)
 RELAY_AFTER = (2, 3, 4)
 LATER = ((), ((3, 1),), ())
 ROUND = tuple(plane for plane, way in DETOUR)

time: 36.1 us -> 36.1 us (level)
  no operation moved by 1% of the time
where the time goes in v7:
time: 36.1 us; the launch traced here: 36 us
  Pallas kernels  35.4 us (98%)
  local copies, waits for them, and re-layouts  0.61 us (2%)
    pallas_call x1, Pallas kernels, local_gradient(): pl.pallas_call(functools.partial(kernel, depth), out_shape=jax.ShapeDtype...  35.4 us

profile of v7, /device:TPU:24, one launch (start us, length us, event | category | flops | bytes accessed | tf_op | source)
XLA Modules:
  0.0 36.0 jit_solution(4101004030400971948)
XLA Ops:
  0.0 35.4 %shard_map.55 = f32[2,3,8,64]{3,2,1,0:T(8,128)S(1)} custom-call(f32[10,40,320]{2,1,0:T(8,128)} %f_hbm.1, f32[10,40,320]{2,1,0:T(8,128)} %m_hbm.1, f32[3,10,40,320]{3,2,1,0:T(8,128)} %g_hbm.1, bf16[384,128]{1,0:T(8,128)(2,1)} %constant.4.clone.bh_hbm, bf16[384,128]{1,0:T(8,128)(2,1)} %constant.5.clone.bl_hbm), custom_call_target="tpu_custom_call" | custom-call | tf_op jit(solution)/shard_map/pallas_call | solution.py:713
  35.4 0.6 %copy.7 = f32[2,3,8,64]{3,2,1,0:T(8,128)} copy(f32[2,3,8,64]{3,2,1,0:T(8,128)S(1)} %shard_map.55) | data formatting | bytes 24576
